TPU v7x, 32 devices: a whole 2x2x4 slice. The times are simulated.
32 devices in a mesh: pb: 4 (over y, x), neg: 8 (over z, core).
Axes of the slice: x: 2, y: 2, z: 4, core: 2. Of those that a mesh axis runs over, the one named last changes fastest.
Arguments:
- hidden: bfloat16 [4, 32, 128, 1024], P('pb', 'neg'), may hold values from -6 to 6
- lengths: int32 [4, 32], P('pb', 'neg'), may hold values from 32 to 128
- teacher: float32 [4, 32], P('pb', 'neg'), may hold values from -8 to 8
- norm_gain: float32 [1024], replicated, may hold values from 0.1 to 1.9
- final_gain: float32 [1024], replicated, may hold values from 0.1 to 1.9
- score_vector: float32 [1024], replicated, may hold values from -0.1875 to 0.1875
- query_weight: bfloat16 [1024, 1024], P(('pb', 'neg')), may hold values from -0.1875 to 0.1875
- key_matrix: bfloat16 [1024, 512], P(('pb', 'neg')), may hold values from -0.1875 to 0.1875
- value_matrix: bfloat16 [1024, 512], P(('pb', 'neg')), may hold values from -0.1875 to 0.1875
- out_weight: bfloat16 [1024, 1024], P(None, ('pb', 'neg')), may hold values from -0.1875 to 0.1875
Outputs:
- scores: float32 [4, 32], P('pb', 'neg')
- loss: float32 [], replicated
- grad_hidden: bfloat16 [4, 32, 128, 1024], P('pb', 'neg')
- grad_query: float32 [1024, 1024], P(('pb', 'neg'))
- grad_key: float32 [1024, 512], P(('pb', 'neg'))
- grad_value: float32 [1024, 512], P(('pb', 'neg'))
- grad_out: float32 [1024, 1024], P(None, ('pb', 'neg'))
Inputs may be any that keep to these rules, and one draw needn't show every extreme that they name: `lengths`: the number of real tokens of the pair; its other positions out of 128 are padding.
All inputs are finite; a program needn't handle non-finite values.
Results may differ from a plain program's by a relative error of at most 0.013.
Values may be sent and summed in bfloat16 or wider, within the bound.
A program may use at most 64 MiB of HBM per device.

v0:
```python
import jax
import jax.numpy as jnp
from jax import lax
from jax.sharding import PartitionSpec as P

HEAD_WIDTH = 128


EPSILON = 1e-06
ROPE_BASE = 1000000.0
TEACHER_TEMP = 2.0
GRAD_SCALE = 512.0


def rope_tables(seq_len, head_size):
    half = head_size // 2
    freqs = ROPE_BASE ** (-(jnp.arange(half, dtype=jnp.float32) * 2.0) / head_size)
    angles = jnp.arange(seq_len, dtype=jnp.float32)[:, None] * freqs[None, :]
    angles = jnp.concatenate([angles, angles], axis=1)
    return (jnp.cos(angles), jnp.sin(angles))


def rotate_half(vector):
    half = vector.shape[-1] // 2
    return jnp.concatenate([-vector[..., half:], vector[..., :half]], axis=-1)


def unrotate_half(vector):
    half = vector.shape[-1] // 2
    return jnp.concatenate([vector[..., half:], -vector[..., :half]], axis=-1)


def forward_pairs(
    tokens_in,
    lengths_here,
    norm_gain,
    final_gain,
    score_vector,
    query_weight,
    key_matrix,
    value_matrix,
    out_weight,
):
    pair_count, seq_len, model_width = tokens_in.shape
    head_count = query_weight.shape[1] // HEAD_WIDTH
    group_count = key_matrix.shape[1] // HEAD_WIDTH
    group_size = head_count // group_count
    inputs_wide = tokens_in.astype(jnp.float32)
    inv_rms = lax.rsqrt(jnp.mean(inputs_wide * inputs_wide, axis=-1, keepdims=True) + EPSILON)
    normed = (inputs_wide * inv_rms * norm_gain).astype(jnp.bfloat16)
    flat_rows = normed.reshape(pair_count * seq_len, model_width)
    key_proj = jnp.dot(flat_rows, key_matrix, preferred_element_type=jnp.float32).reshape(
        pair_count, seq_len, group_count, HEAD_WIDTH
    )
    value_proj = jnp.dot(flat_rows, value_matrix, preferred_element_type=jnp.float32).reshape(
        pair_count, seq_len, group_count, HEAD_WIDTH
    )
    positions = jnp.arange(seq_len, dtype=jnp.int32)
    last_index = lengths_here - 1
    onehot = (positions[None, :] == last_index[:, None]).astype(jnp.float32)
    normed_last = jnp.take_along_axis(normed, last_index[:, None, None], axis=1)[:, 0]
    query_proj = jnp.dot(normed_last, query_weight, preferred_element_type=jnp.float32).reshape(
        pair_count, head_count, HEAD_WIDTH
    )
    query_scale = lax.rsqrt(jnp.mean(query_proj * query_proj, axis=-1, keepdims=True) + EPSILON)
    query_unit = query_proj * query_scale
    key_scale = lax.rsqrt(jnp.mean(key_proj * key_proj, axis=-1, keepdims=True) + EPSILON)
    key_unit = key_proj * key_scale
    cos_table, sin_table = rope_tables(seq_len, HEAD_WIDTH)
    cos_query = jnp.dot(onehot, cos_table, precision=lax.Precision.HIGHEST)
    sin_query = jnp.dot(onehot, sin_table, precision=lax.Precision.HIGHEST)
    query_rot = (
        query_unit * cos_query[:, None, :] + rotate_half(query_unit) * sin_query[:, None, :]
    ).astype(jnp.bfloat16)
    key_rot = (
        key_unit * cos_table[None, :, None, :] + rotate_half(key_unit) * sin_table[None, :, None, :]
    ).astype(jnp.bfloat16)
    value_cast = value_proj.astype(jnp.bfloat16)
    grouped = query_rot.reshape(pair_count, group_count, group_size, HEAD_WIDTH)
    logits = jnp.einsum(
        "pkgd,pskd->pkgs", grouped, key_rot, preferred_element_type=jnp.float32
    ) * HEAD_WIDTH ** (-0.5)
    visible = (positions[None, :] <= last_index[:, None])[:, None, None, :]
    expos = jnp.where(visible, jnp.exp(logits), 0.0)
    attention_weights = expos / jnp.sum(expos, axis=-1, keepdims=True)
    probs_cast = attention_weights.astype(jnp.bfloat16)
    context = jnp.einsum(
        "pkgs,pskd->pkgd", probs_cast, value_cast, preferred_element_type=jnp.float32
    )
    context = context.astype(jnp.bfloat16).reshape(pair_count, head_count * HEAD_WIDTH)
    attended = jnp.dot(context, out_weight, preferred_element_type=jnp.float32)
    residual = jnp.take_along_axis(inputs_wide, last_index[:, None, None], axis=1)[:, 0] + attended
    out_scale = lax.rsqrt(jnp.mean(residual * residual, axis=-1, keepdims=True) + EPSILON)
    out_unit = residual * out_scale
    scores_here = jnp.sum(out_unit * final_gain * score_vector, axis=-1)
    stored = (
        tokens_in,
        onehot,
        inv_rms,
        normed,
        normed_last,
        query_unit,
        query_scale,
        key_unit,
        key_scale,
        cos_query,
        sin_query,
        cos_table,
        sin_table,
        query_rot,
        key_rot,
        value_cast,
        attention_weights,
        probs_cast,
        context,
        out_unit,
        out_scale,
    )
    return (scores_here, stored)


def backward_pairs(
    stored,
    grad_score,
    norm_gain,
    final_gain,
    score_vector,
    query_weight,
    key_matrix,
    value_matrix,
    out_weight,
):
    (
        tokens_in,
        onehot,
        inv_rms,
        normed,
        normed_last,
        query_unit,
        query_scale,
        key_unit,
        key_scale,
        cos_query,
        sin_query,
        cos_table,
        sin_table,
        query_rot,
        key_rot,
        value_cast,
        attention_weights,
        probs_cast,
        context,
        out_unit,
        out_scale,
    ) = stored
    pair_count, seq_len, model_width = tokens_in.shape
    head_count = query_weight.shape[1] // HEAD_WIDTH
    group_count = key_matrix.shape[1] // HEAD_WIDTH
    group_size = head_count // group_count
    grad_unit = grad_score[:, None] * score_vector * final_gain
    grad_resid = out_scale * (
        grad_unit - out_unit * jnp.mean(grad_unit * out_unit, axis=-1, keepdims=True)
    )
    grad_resid_cast = grad_resid.astype(jnp.bfloat16)
    grad_out = jnp.dot(context.T, grad_resid_cast, preferred_element_type=jnp.float32)
    grad_context = jnp.dot(
        grad_resid_cast, out_weight.T, preferred_element_type=jnp.float32
    ).astype(jnp.bfloat16)
    grad_context = grad_context.reshape(pair_count, group_count, group_size, HEAD_WIDTH)
    grad_probs = jnp.einsum(
        "pkgd,pskd->pkgs", grad_context, value_cast, preferred_element_type=jnp.float32
    )
    grad_vals = jnp.einsum(
        "pkgs,pkgd->pskd", probs_cast, grad_context, preferred_element_type=jnp.float32
    )
    spread = jnp.sum(attention_weights * grad_probs, axis=-1, keepdims=True)
    logit_gradient = (attention_weights * (grad_probs - spread)).astype(jnp.bfloat16)
    grouped = query_rot.reshape(pair_count, group_count, group_size, HEAD_WIDTH)
    rotated_query_gradient = jnp.einsum(
        "pkgs,pskd->pkgd", logit_gradient, key_rot, preferred_element_type=jnp.float32
    ) * HEAD_WIDTH ** (-0.5)
    rotated_query_gradient = rotated_query_gradient.reshape(pair_count, head_count, HEAD_WIDTH)
    grad_krot = jnp.einsum(
        "pkgs,pkgd->pskd", logit_gradient, grouped, preferred_element_type=jnp.float32
    ) * HEAD_WIDTH ** (-0.5)
    grad_qunit = rotated_query_gradient * cos_query[:, None, :] + unrotate_half(
        rotated_query_gradient * sin_query[:, None, :]
    )
    grad_kunit = grad_krot * cos_table[None, :, None, :] + unrotate_half(
        grad_krot * sin_table[None, :, None, :]
    )
    grad_qproj = query_scale * (
        grad_qunit - query_unit * jnp.mean(grad_qunit * query_unit, axis=-1, keepdims=True)
    )
    grad_kproj = key_scale * (
        grad_kunit - key_unit * jnp.mean(grad_kunit * key_unit, axis=-1, keepdims=True)
    )
    grad_q_cast = grad_qproj.reshape(pair_count, head_count * HEAD_WIDTH).astype(jnp.bfloat16)
    grad_k_cast = grad_kproj.reshape(pair_count * seq_len, group_count * HEAD_WIDTH).astype(
        jnp.bfloat16
    )
    grad_v_cast = grad_vals.reshape(pair_count * seq_len, group_count * HEAD_WIDTH).astype(
        jnp.bfloat16
    )
    flat_rows = normed.reshape(pair_count * seq_len, model_width)
    grad_query = jnp.dot(normed_last.T, grad_q_cast, preferred_element_type=jnp.float32)
    grad_key = jnp.dot(flat_rows.T, grad_k_cast, preferred_element_type=jnp.float32)
    grad_value = jnp.dot(flat_rows.T, grad_v_cast, preferred_element_type=jnp.float32)
    grad_normed = jnp.dot(grad_k_cast, key_matrix.T, preferred_element_type=jnp.float32)
    grad_normed = grad_normed + jnp.dot(
        grad_v_cast, value_matrix.T, preferred_element_type=jnp.float32
    )
    grad_normed = grad_normed.reshape(pair_count, seq_len, model_width)
    grad_last = jnp.dot(grad_q_cast, query_weight.T, preferred_element_type=jnp.float32)
    grad_normed = grad_normed + onehot[:, :, None] * grad_last[:, None, :]
    inputs_wide = tokens_in.astype(jnp.float32)
    grad_scaled = grad_normed * norm_gain
    grad_input = inv_rms * grad_scaled - inputs_wide * inv_rms * inv_rms * inv_rms * jnp.mean(
        grad_scaled * inputs_wide, axis=-1, keepdims=True
    )
    grad_input = grad_input + onehot[:, :, None] * grad_resid[:, None, :]
    return (grad_input.astype(jnp.bfloat16), (grad_query, grad_key, grad_value, grad_out))


def shards(
    hidden,
    lengths,
    teacher,
    norm_gain,
    final_gain,
    score_vector,
    query_weight,
    key_matrix,
    value_matrix,
    out_weight,
):
    tokens_in = hidden[0]
    lengths_here = lengths[0]
    gathered = (
        lax.all_gather(query_weight, ("pb", "neg"), axis=0, tiled=True),
        lax.all_gather(key_matrix, ("pb", "neg"), axis=0, tiled=True),
        lax.all_gather(value_matrix, ("pb", "neg"), axis=0, tiled=True),
        lax.all_gather(out_weight, ("pb", "neg"), axis=1, tiled=True),
    )
    scores_here, stored = forward_pairs(
        tokens_in,
        lengths_here,
        norm_gain,
        final_gain,
        score_vector,
        gathered[0],
        gathered[1],
        gathered[2],
        gathered[3],
    )
    scaled = teacher[0] / TEACHER_TEMP
    expo_s = jnp.exp(scores_here)
    expo_t = jnp.exp(scaled)
    total_s, total_t = lax.psum((jnp.sum(expo_s), jnp.sum(expo_t)), "neg")
    prob_s = expo_s / total_s
    prob_t = expo_t / total_t
    local_terms = jnp.sum(prob_t * (scaled - jnp.log(total_t) - (scores_here - jnp.log(total_s))))
    loss_value = lax.psum(local_terms, ("pb", "neg"))
    grad_score = GRAD_SCALE * (prob_s - prob_t)
    weights_back = (
        lax.all_gather(query_weight, ("pb", "neg"), axis=0, tiled=True),
        lax.all_gather(key_matrix, ("pb", "neg"), axis=0, tiled=True),
        lax.all_gather(value_matrix, ("pb", "neg"), axis=0, tiled=True),
        lax.all_gather(out_weight, ("pb", "neg"), axis=1, tiled=True),
    )
    grad_input, grads = backward_pairs(
        stored,
        grad_score,
        norm_gain,
        final_gain,
        score_vector,
        weights_back[0],
        weights_back[1],
        weights_back[2],
        weights_back[3],
    )
    by_query = (
        lax.psum_scatter(
            grads[0].astype(jnp.bfloat16), "pb", scatter_dimension=0, tiled=True
        ).astype(jnp.float32),
        lax.psum_scatter(
            grads[1].astype(jnp.bfloat16), "pb", scatter_dimension=0, tiled=True
        ).astype(jnp.float32),
        lax.psum_scatter(
            grads[2].astype(jnp.bfloat16), "pb", scatter_dimension=0, tiled=True
        ).astype(jnp.float32),
        lax.psum_scatter(
            grads[3].astype(jnp.bfloat16), "pb", scatter_dimension=1, tiled=True
        ).astype(jnp.float32),
    )
    reduced = (
        lax.psum_scatter(by_query[0], "neg", scatter_dimension=0, tiled=True),
        lax.psum_scatter(by_query[1], "neg", scatter_dimension=0, tiled=True),
        lax.psum_scatter(by_query[2], "neg", scatter_dimension=0, tiled=True),
        lax.psum_scatter(by_query[3], "neg", scatter_dimension=1, tiled=True),
    )
    return (
        scores_here[None],
        loss_value,
        grad_input[None],
        reduced[0],
        reduced[1],
        reduced[2],
        reduced[3],
    )


def solution(mesh):
    placed = (
        P("pb", "neg", None, None),
        P("pb", "neg"),
        P("pb", "neg"),
        P(),
        P(),
        P(),
        P(("pb", "neg"), None),
        P(("pb", "neg"), None),
        P(("pb", "neg"), None),
        P(None, ("pb", "neg")),
    )
    return jax.shard_map(
        shards,
        mesh=mesh,
        in_specs=placed,
        out_specs=(
            P("pb", "neg"),
            P(),
            P("pb", "neg", None, None),
            P(("pb", "neg"), None),
            P(("pb", "neg"), None),
            P(("pb", "neg"), None),
            P(None, ("pb", "neg")),
        ),
        check_vma=False,
    )
```

profile of v0, /device:TPU:0, one launch (start us, length us, event | category | flops | bytes accessed | tf_op | source)
XLA Modules:
  0.0 541.0 jit_solution(14512018428589299706)
XLA Ops:
  12.0 1.6 multiply_reduce_fusion
  13.6 1.5 convert_bitcast_fusion
  17.1 1.4 gather_fusion.1
  21.6 45.9 %all-gather.9.cloned.1.call-done = bf16[1024,512]{1,0:T(8,128)(2,1)} async-done(((bf16[32,512]{1,0:T(8,128)(2,1)}), bf16[1024,512]{1,0:T(8,128)(2,1)}) %all-gather.9.cloned.1.call-update) | async-done | bytes 1048592 | tf_op jit(solution)/shard_map/all_gather | solution.py:242
  67.6 2.3 copy.41
  69.8 53.6 %all-gather.7.cloned.1.call-done = bf16[1024,512]{1,0:T(8,128)(2,1)} async-done(((bf16[32,512]{1,0:T(8,128)(2,1)}), bf16[1024,512]{1,0:T(8,128)(2,1)}) %all-gather.7.cloned.1.call-update) | async-done | bytes 1048592 | tf_op jit(solution)/shard_map/all_gather | solution.py:241
  123.4 2.3 copy.38
  125.7 2.3 multiply_reduce_fusion.2
  130.4 51.4 %all-gather.5.cloned.1.call-done = bf16[1024,1024]{1,0:T(8,128)(2,1)} async-done(((bf16[32,1024]{1,0:T(8,128)(2,1)}), bf16[1024,1024]{1,0:T(8,128)(2,1)}) %all-gather.5.cloned.1.call-update) | async-done | bytes 2097168 | tf_op jit(solution)/shard_map/all_gather | solution.py:240
  181.8 3.9 copy.37
  185.7 2.3 multiply_reduce_fusion.8
  188.9 50.9 %all-gather.11.cloned.1.call-done = bf16[1024,1024]{0,1:T(8,128)(2,1)} async-done(((bf16[1024,32]{0,1:T(8,128)(2,1)}), bf16[1024,1024]{0,1:T(8,128)(2,1)}) %all-gather.11.cloned.1.call-update) | async-done | bytes 2097168 | tf_op jit(solution)/shard_map/all_gather | solution.py:243
  239.9 2.4 multiply_reduce_fusion.7
  243.0 16.2 %all-reduce = (f32[]{:T(128)}, f32[]{:T(128)}) all-reduce(f32[]{:T(128)} %exponential_reduce_fusion.1, f32[]{:T(128)} %exponential_reduce_fusion), channel_id=1, replica_groups=mesh['pb'=4,'neg'=8] {'neg'}, use_global_device_ids=true, to_apply=%region_7.8 | all-reduce | flops 2 | bytes 16 | tf_op jit(solution)/shard_map/psum | solution.py:259
  260.8 2.0 convolution_convert_fusion.6
  265.0 3.1 convolution_convert_fusion.3
  268.9 3.1 convolution_convert_fusion.2
  273.0 2.1 convolution_convert_fusion.1
  275.2 2.1 convolution_convert_fusion
  277.5 15.9 %reduce-scatter.15.cloned.1.call-done = bf16[256,512]{1,0:T(8,128)(2,1)} async-done(((bf16[1024,512]{1,0:T(8,128)(2,1)}), bf16[256,512]{1,0:T(8,128)(2,1)}) %reduce-scatter.15.cloned.1.call-update) | async-done | bytes 262160 | tf_op jit(solution)/shard_map/reduce_scatter | solution.py:286
  293.4 1.9 convert_element_type.170
  295.4 28.8 %reduce-scatter.19.cloned.1.call-done = bf16[256,512]{1,0:T(8,128)(2,1)} async-done(((bf16[1024,512]{1,0:T(8,128)(2,1)}), bf16[256,512]{1,0:T(8,128)(2,1)}) %reduce-scatter.19.cloned.1.call-update) | async-done | bytes 262160 | tf_op jit(solution)/shard_map/reduce_scatter | solution.py:289
  324.1 1.9 convert_element_type.172
  326.1 36.2 %reduce-scatter.11.cloned.1.call-done = bf16[256,1024]{1,0:T(8,128)(2,1)} async-done(((bf16[1024,1024]{1,0:T(8,128)(2,1)}), bf16[256,1024]{1,0:T(8,128)(2,1)}) %reduce-scatter.11.cloned.1.call-update) | async-done | bytes 524304 | tf_op jit(solution)/shard_map/reduce_scatter | solution.py:283
  362.3 2.1 convert_element_type.167
  364.5 36.0 %reduce-scatter.23.cloned.1.call-done = bf16[1024,256]{1,0:T(8,128)(2,1)} async-done(((bf16[1024,1024]{1,0:T(8,128)(2,1)}), bf16[1024,256]{1,0:T(8,128)(2,1)}) %reduce-scatter.23.cloned.1.call-update) | async-done | bytes 524304 | tf_op jit(solution)/shard_map/reduce_scatter | solution.py:292
  400.5 2.3 copy.51
  404.7 39.8 %psum.23 = f32[]{:T(128)} all-reduce(f32[]{:T(128)} %fusion.44), channel_id=1, replica_groups=mesh['pb'=4,'neg'=8] {'pb','neg'}, use_global_device_ids=true, to_apply=%region_11.12 | all-reduce | flops 1 | bytes 8 | tf_op jit(solution)/shard_map/psum | solution.py:263
  448.3 2.5 add_convert_fusion
  450.8 16.3 %reduce-scatter.21.cloned.1.call-done = f32[32,512]{1,0:T(8,128)} async-done(((f32[256,512]{1,0:T(8,128)}), f32[32,512]{1,0:T(8,128)}) %reduce-scatter.21.cloned.1.call-update) | async-done | bytes 65552 | tf_op jit(solution)/shard_map/reduce_scatter | solution.py:299
  467.0 33.6 %reduce-scatter.13.cloned.1.call-done = f32[32,1024]{1,0:T(8,128)} async-done(((f32[256,1024]{1,0:T(8,128)}), f32[32,1024]{1,0:T(8,128)}) %reduce-scatter.13.cloned.1.call-update) | async-done | bytes 131088 | tf_op jit(solution)/shard_map/reduce_scatter | solution.py:297
  500.7 33.5 %reduce-scatter.25.cloned.1.call-done = f32[32,1024]{1,0:T(8,128)} async-done(((f32[256,1024]{1,0:T(8,128)}), f32[32,1024]{1,0:T(8,128)}) %reduce-scatter.25.cloned.1.call-update) | async-done | bytes 131088
  (116 shorter events, 24.0 us)
Async XLA Ops:
  7.2 60.4 %all-gather.9.cloned.1.call-start = ((), (), s32[]{:S(2)}) async-start(), calls=%async_computation.10 | async-start | bytes 1081344 | tf_op jit(solution)/shard_map/all_gather | solution.py:242
  7.9 115.5 %all-gather.7.cloned.1.call-start = ((), (), s32[]{:S(2)}) async-start(), calls=%async_computation.9 | async-start | bytes 1081344 | tf_op jit(solution)/shard_map/all_gather | solution.py:241
  8.6 173.1 %all-gather.5.cloned.1.call-start = ((), (), s32[]{:S(2)}) async-start(), calls=%async_computation.8 | async-start | bytes 2162688 | tf_op jit(solution)/shard_map/all_gather | solution.py:240
  9.4 230.5 %all-gather.11.cloned.1.call-start = ((), (), s32[]{:S(2)}) async-start(), calls=%async_computation.11 | async-start | bytes 2162688 | tf_op jit(solution)/shard_map/all_gather | solution.py:243
  10.0 283.5 %reduce-scatter.15.cloned.1.call-start = ((), (), s32[]{:S(2)}) async-start(), calls=%async_computation.14 | async-start | bytes 1310720 | tf_op jit(solution)/shard_map/reduce_scatter | solution.py:286
  12.0 3.8 copy-start
  12.0 3.8 copy-start.10
  15.1 4.1 copy-start.14
  128.1 1.2 copy-start.8
  128.1 1.5 copy-start.9
  188.0 54.2 %copy-start.11 = (f32[1024]{0:T(1024)S(1)}, f32[1024]{0:T(1024)}, u32[]{:S(2)}) copy-start(f32[1024]{0:T(1024)} %param.15) | copy-start | bytes 12292
  188.0 54.2 %copy-start.12 = (f32[1024]{0:T(1024)S(1)}, f32[1024]{0:T(1024)}, u32[]{:S(2)}) copy-start(f32[1024]{0:T(1024)} %param.14) | copy-start | bytes 12292
  242.4 161.7 %copy-start.13 = (f32[4]{0:T(128)}, f32[4]{0:T(128)S(1)}, u32[]{:S(2)}) copy-start(f32[4]{0:T(128)S(1)} %multiply_reduce_fusion.6) | copy-start | bytes 52
  265.0 3.2 copy-start.4
  268.1 56.0 %reduce-scatter.19.cloned.1.call-start = ((), (), s32[]{:S(2)}) async-start(), calls=%async_computation.16 | async-start | bytes 1310720 | tf_op jit(solution)/shard_map/reduce_scatter | solution.py:289
  268.9 3.2 copy-start.6
  272.1 90.2 %reduce-scatter.11.cloned.1.call-start = ((), (), s32[]{:S(2)}) async-start(), calls=%async_computation.12 | async-start | bytes 2621440 | tf_op jit(solution)/shard_map/reduce_scatter | solution.py:283
  275.2 125.3 %reduce-scatter.23.cloned.1.call-start = ((), (), s32[]{:S(2)}) async-start(), calls=%async_computation.18 | async-start | bytes 2621440 | tf_op jit(solution)/shard_map/reduce_scatter | solution.py:292
  277.3 173.5 %reduce-scatter.17.cloned.1.call-start = ((), (), s32[]{:S(2)}) async-start(), calls=%async_computation.15 | async-start | bytes 589824 | tf_op jit(solution)/shard_map/reduce_scatter | solution.py:298
  295.3 171.7 %reduce-scatter.21.cloned.1.call-start = ((), (), s32[]{:S(2)}) async-start(), calls=%async_computation.17 | async-start | bytes 589824 | tf_op jit(solution)/shard_map/reduce_scatter | solution.py:299
  326.0 174.6 %reduce-scatter.13.cloned.1.call-start = ((), (), s32[]{:S(2)}) async-start(), calls=%async_computation.13 | async-start | bytes 1179648 | tf_op jit(solution)/shard_map/reduce_scatter | solution.py:297
  364.5 80.1 %copy-start.1 = (bf16[1024,1024]{1,0:T(8,128)(2,1)S(1)}, bf16[1024,1024]{1,0:T(8,128)(2,1)}, u32[]{:S(2)}) copy-start(bf16[1024,1024]{1,0:T(8,128)(2,1)} %all-gather.5.cloned.1.call-done) | copy-start | bytes 6291460
  364.5 169.7 %reduce-scatter.25.cloned.1.call-start = ((), (), s32[]{:S(2)}) async-start(), calls=%async_computation.19 | async-start | bytes 1179648
  444.5 1.2 copy-start.2
  444.5 1.4 copy-start.5
  445.9 1.2 copy-start.3
  445.9 1.4 copy-start.7
Sparse Core Ops, SparseCore 0:
  11.0 56.5 all-gather.8
  70.5 52.7 all-gather.6
  126.4 55.3 all-gather.4
  184.6 55.2 all-gather.10
  268.2 25.1 reduce-scatter.14
  296.2 27.9 reduce-scatter.18
  327.1 35.1 reduce-scatter.10
  365.3 35.1 reduce-scatter.22
  403.3 31.4 reduce-scatter.16
  437.5 29.4 reduce-scatter.20
  469.9 30.7 reduce-scatter.12
  503.4 30.7 reduce-scatter.24
where the time goes:
time: 542 us; the launch traced here: 541 us
  waiting for transfers between devices  405 us (75%)
  blocking collectives  56 us (10%)
  matrix products  25.4 us (5%)
  other arithmetic  22.2 us (4%)
  local copies, waits for them, and re-layouts  16 us (3%)
  between operations  15.9 us (3%)
    all_gather x1, waiting for transfers between devices, shards(): lax.all_gather(key_matrix, ('pb', 'neg'), axis=0, tiled=True)  53.6 us
    all_gather x1, waiting for transfers between devices, shards(): lax.all_gather(query_weight, ('pb', 'neg'), axis=0, tiled=True)  51.4 us
    all_gather x1, waiting for transfers between devices, shards(): lax.all_gather(out_weight, ('pb', 'neg'), axis=1, tiled=True)  50.9 us
    all_gather x1, waiting for transfers between devices, shards(): lax.all_gather(value_matrix, ('pb', 'neg'), axis=0, tiled=True)  45.9 us
    psum x1, blocking collectives, shards(): loss_value = lax.psum(local_terms, ('pb', 'neg'))  39.8 us
    reduce_scatter x1, waiting for transfers between devices, shards(): lax.psum_scatter(grads[0].astype(jnp.bfloat16), 'pb', scatter_dimension=0...  36.2 us
    unnamed x13, waiting for transfers between devices  36.2 us
    reduce_scatter x1, waiting for transfers between devices, shards(): lax.psum_scatter(grads[3].astype(jnp.bfloat16), 'pb', scatter_dimension=1...  36 us
  transfers between devices with their start and end apart: 12, of which 11 were waited for; matrix products, arithmetic and copies ran while one was open for 9% of the time, Pallas kernels for 0%

commit v1 on v0

--- a/solution.py
+++ b/solution.py
@@ -162,7 +162,6 @@
         grad_unit - out_unit * jnp.mean(grad_unit * out_unit, axis=-1, keepdims=True)
     )
     grad_resid_cast = grad_resid.astype(jnp.bfloat16)
-    grad_out = jnp.dot(context.T, grad_resid_cast, preferred_element_type=jnp.float32)
     grad_context = jnp.dot(
         grad_resid_cast, out_weight.T, preferred_element_type=jnp.float32
     ).astype(jnp.bfloat16)
@@ -203,9 +202,12 @@
         jnp.bfloat16
     )
     flat_rows = normed.reshape(pair_count * seq_len, model_width)
-    grad_query = jnp.dot(normed_last.T, grad_q_cast, preferred_element_type=jnp.float32)
-    grad_key = jnp.dot(flat_rows.T, grad_k_cast, preferred_element_type=jnp.float32)
-    grad_value = jnp.dot(flat_rows.T, grad_v_cast, preferred_element_type=jnp.float32)
+    last_rows = jnp.concatenate([normed_last, grad_resid_cast, grad_q_cast, context], axis=1)
+    grad_kv = jnp.dot(
+        flat_rows.T,
+        jnp.concatenate([grad_k_cast, grad_v_cast], axis=1),
+        preferred_element_type=jnp.float32,
+    )
     grad_normed = jnp.dot(grad_k_cast, key_matrix.T, preferred_element_type=jnp.float32)
     grad_normed = grad_normed + jnp.dot(
         grad_v_cast, value_matrix.T, preferred_element_type=jnp.float32
@@ -219,7 +221,7 @@
         grad_scaled * inputs_wide, axis=-1, keepdims=True
     )
     grad_input = grad_input + onehot[:, :, None] * grad_resid[:, None, :]
-    return (grad_input.astype(jnp.bfloat16), (grad_query, grad_key, grad_value, grad_out))
+    return (grad_input.astype(jnp.bfloat16), last_rows, grad_kv)
 
 
 def shards(
@@ -234,79 +236,80 @@
     value_matrix,
     out_weight,
 ):
-    tokens_in = hidden[0]
-    lengths_here = lengths[0]
-    gathered = (
-        lax.all_gather(query_weight, ("pb", "neg"), axis=0, tiled=True),
-        lax.all_gather(key_matrix, ("pb", "neg"), axis=0, tiled=True),
-        lax.all_gather(value_matrix, ("pb", "neg"), axis=0, tiled=True),
-        lax.all_gather(out_weight, ("pb", "neg"), axis=1, tiled=True),
-    )
+    both = ("pb", "neg")
+    width = query_weight.shape[1]
+    kv_width = key_matrix.shape[1]
+    head_width = out_weight.shape[0]
+    packed = jnp.concatenate([query_weight, key_matrix, value_matrix, out_weight.T], axis=1)
+    everything = lax.all_gather(packed, both, axis=0, tiled=True)
+    full_query = everything[:, :width]
+    full_key = everything[:, width : width + kv_width]
+    full_value = everything[:, width + kv_width : width + 2 * kv_width]
+    full_out_t = everything[:, width + 2 * kv_width :]
     scores_here, stored = forward_pairs(
-        tokens_in,
-        lengths_here,
+        hidden[0],
+        lengths[0],
         norm_gain,
         final_gain,
         score_vector,
-        gathered[0],
-        gathered[1],
-        gathered[2],
-        gathered[3],
-    )
-    scaled = teacher[0] / TEACHER_TEMP
-    expo_s = jnp.exp(scores_here)
-    expo_t = jnp.exp(scaled)
-    total_s, total_t = lax.psum((jnp.sum(expo_s), jnp.sum(expo_t)), "neg")
-    prob_s = expo_s / total_s
-    prob_t = expo_t / total_t
-    local_terms = jnp.sum(prob_t * (scaled - jnp.log(total_t) - (scores_here - jnp.log(total_s))))
-    loss_value = lax.psum(local_terms, ("pb", "neg"))
+        full_query,
+        full_key,
+        full_value,
+        full_out_t.T,
+    )
+    pair_count = scores_here.shape[0]
+    row = lax.axis_index("pb")
+    listed = lax.all_gather(jnp.concatenate([scores_here, teacher[0]])[None], both, axis=0, tiled=True)
+    listed = listed.reshape(lax.axis_size("pb"), -1, 2, pair_count)
+    all_scores = listed[:, :, 0].reshape(listed.shape[0], -1)
+    all_scaled = listed[:, :, 1].reshape(listed.shape[0], -1) / TEACHER_TEMP
+    total_s = jnp.sum(jnp.exp(all_scores), axis=1, keepdims=True)
+    expo_t = jnp.exp(all_scaled)
+    total_t = jnp.sum(expo_t, axis=1, keepdims=True)
+    loss_value = jnp.sum(
+        expo_t
+        / total_t
+        * (all_scaled - jnp.log(total_t) - (all_scores - jnp.log(total_s)))
+    )
+    mine = (jnp.arange(listed.shape[0]) == row)[:, None]
+    my_total_s = jnp.sum(jnp.where(mine, total_s, 0.0))
+    my_total_t = jnp.sum(jnp.where(mine, total_t, 0.0))
+    prob_s = jnp.exp(scores_here) / my_total_s
+    prob_t = jnp.exp(teacher[0] / TEACHER_TEMP) / my_total_t
     grad_score = GRAD_SCALE * (prob_s - prob_t)
-    weights_back = (
-        lax.all_gather(query_weight, ("pb", "neg"), axis=0, tiled=True),
-        lax.all_gather(key_matrix, ("pb", "neg"), axis=0, tiled=True),
-        lax.all_gather(value_matrix, ("pb", "neg"), axis=0, tiled=True),
-        lax.all_gather(out_weight, ("pb", "neg"), axis=1, tiled=True),
-    )
-    grad_input, grads = backward_pairs(
+    grad_input, last_rows, grad_kv = backward_pairs(
         stored,
         grad_score,
         norm_gain,
         final_gain,
         score_vector,
-        weights_back[0],
-        weights_back[1],
-        weights_back[2],
-        weights_back[3],
-    )
-    by_query = (
-        lax.psum_scatter(
-            grads[0].astype(jnp.bfloat16), "pb", scatter_dimension=0, tiled=True
-        ).astype(jnp.float32),
-        lax.psum_scatter(
-            grads[1].astype(jnp.bfloat16), "pb", scatter_dimension=0, tiled=True
-        ).astype(jnp.float32),
-        lax.psum_scatter(
-            grads[2].astype(jnp.bfloat16), "pb", scatter_dimension=0, tiled=True
-        ).astype(jnp.float32),
-        lax.psum_scatter(
-            grads[3].astype(jnp.bfloat16), "pb", scatter_dimension=1, tiled=True
-        ).astype(jnp.float32),
-    )
-    reduced = (
-        lax.psum_scatter(by_query[0], "neg", scatter_dimension=0, tiled=True),
-        lax.psum_scatter(by_query[1], "neg", scatter_dimension=0, tiled=True),
-        lax.psum_scatter(by_query[2], "neg", scatter_dimension=0, tiled=True),
-        lax.psum_scatter(by_query[3], "neg", scatter_dimension=1, tiled=True),
-    )
+        full_query,
+        full_key,
+        full_value,
+        full_out_t.T,
+    )
+    reduced = lax.psum_scatter(grad_kv.astype(jnp.bfloat16), both, scatter_dimension=0, tiled=True)
+    reduced = reduced.astype(jnp.float32)
+    rows = lax.all_gather(last_rows, both, axis=0, tiled=True)
+    index = row * lax.axis_size("neg") + lax.axis_index("neg")
+    share = query_weight.shape[0]
+    model_width = share * lax.axis_size("pb") * lax.axis_size("neg")
+    out_share = out_weight.shape[1]
+    normed_cols = lax.dynamic_slice_in_dim(rows, index * share, share, axis=1)
+    resid_cols = lax.dynamic_slice_in_dim(rows, model_width + index * out_share, out_share, axis=1)
+    rest = 2 * model_width
+    all_q = rows[:, rest : rest + width]
+    all_context = rows[:, rest + width :]
+    grad_query = jnp.dot(normed_cols.T, all_q, preferred_element_type=jnp.float32)
+    grad_out = jnp.dot(all_context.T, resid_cols, preferred_element_type=jnp.float32)
     return (
         scores_here[None],
         loss_value,
         grad_input[None],
-        reduced[0],
-        reduced[1],
-        reduced[2],
-        reduced[3],
+        grad_query,
+        reduced[:, :kv_width],
+        reduced[:, kv_width:],
+        grad_out,
     )
 
 

time: 542 us -> 354 us (0.65)
  waiting for transfers between devices: 405 us -> 238 us
  blocking collectives: 56 us -> 39.2 us
    all_gather x4 -> x2, waiting for transfers between devices: 202 us -> 102 us  [the longest x1 68.7 us: shards(): everything = lax.all_gather(packed, both, axis=0, tiled=True)]
    psum x2 -> x0, blocking collectives: 56 us -> none  [the longest x1 39.8 us: shards(): loss_value = lax.psum(local_terms, ('pb', 'neg'))]
    unnamed x0 -> x1, blocking collectives: none -> 39.2 us
    unnamed x13 -> x3, waiting for transfers between devices: 36.2 us -> 0.05 us
    reduce_scatter x7 -> x1, waiting for transfers between devices: 167 us -> 137 us  [shards(): lax.psum_scatter(grad_kv.astype(jnp.bfloat16), both, scatter_dimension=0,...]
    dot_general x4 -> x3, matrix products: 10.5 us -> 4.53 us  [the longest x1 2.65 us: backward_pairs(): jnp.dot(flat_rows.T, jnp.concatenate([grad_k_cast, grad_v_cast], axis=1),...]
    convert_element_type x4 -> x2, other arithmetic: 8.33 us -> 2.49 us  [the longest x1 2.41 us: backward_pairs(): return (grad_input.astype(jnp.bfloat16), last_rows, grad_kv)]
  transfers between devices with their start and end apart: 12 -> 3, of which waited for: 11 -> 3; matrix products, arithmetic and copies ran while one was open for 9% -> 9% of each run, Pallas kernels for 0% -> 0%
where the time goes in v1:
time: 354 us
  waiting for transfers between devices  238 us (67%)
  blocking collectives  39.2 us (11%)
  matrix products  25 us (7%)
  local copies, waits for them, and re-layouts  19.3 us (5%)
  other arithmetic  17.3 us (5%)
  between operations  14.2 us (4%)
    reduce_scatter x1, waiting for transfers between devices, shards(): lax.psum_scatter(grad_kv.astype(jnp.bfloat16), both, scatter_dimension=0,...  137 us
    all_gather x1, waiting for transfers between devices, shards(): everything = lax.all_gather(packed, both, axis=0, tiled=True)  68.7 us
    unnamed x1, blocking collectives  39.2 us
    all_gather x1, waiting for transfers between devices, shards(): rows = lax.all_gather(last_rows, both, axis=0, tiled=True)  32.8 us
  transfers between devices with their start and end apart: 3, of which 3 were waited for; matrix products, arithmetic and copies ran while one was open for 9% of the time, Pallas kernels for 0%

profile of v1, /device:TPU:0, one launch (start us, length us, event | category | flops | bytes accessed | tf_op | source)
XLA Modules:
  0.0 353.5 jit_solution(12896501408569046601)
XLA Ops:
  7.2 1.7 pad_maximum_fusion
  9.7 1.5 multiply_reduce_fusion
  11.2 1.0 multiply_convert_fusion
  14.9 68.7 %all-gather.5.cloned.1.call-done = bf16[1024,3072]{1,0:T(8,128)(2,1)} async-done(((bf16[32,3072]{1,0:T(8,128)(2,1)}), bf16[1024,3072]{1,0:T(8,128)(2,1)}) %all-gather.5.cloned.1.call-update) | async-done | bytes 6291472 | tf_op jit(solution)/shard_map/all_gather | solution.py:244
  83.6 3.1 slice_bitcast_fusion
  86.7 2.9 copy.45
  90.5 1.7 slice_bitcast_fusion.2
  92.2 1.3 copy.46
  93.5 2.1 multiply_reduce_fusion.2
  95.7 1.1 slice_negate_fusion.1
  96.8 1.3 copy.49
  98.2 2.1 convolution_convert_fusion.2
  101.2 2.4 multiply_reduce_fusion.7
  104.0 39.2 %all-reduce = f32[256]{0:T(256)S(1)} all-reduce(f32[256]{0:T(256)S(1)} %maximum_dynamic-update-slice_fusion), channel_id=2, replica_groups=mesh['pb'=4,'neg'=8] {'pb','neg'}, use_global_device_ids=true, to_apply=%add | all-reduce | flops 256 | bytes 2048
  144.3 1.3 fusion.73
  145.9 2.0 fusion.25
  149.0 1.3 broadcast_multiply_fusion
  151.6 1.2 fusion.19
  152.8 2.1 copy.54
  155.0 1.3 fusion.83
  156.6 1.1 multiply_convert_fusion.1
  157.7 1.3 copy.53
  159.1 1.1 copy.76
  160.3 2.2 fusion.17
  162.5 2.0 fusion.35
  164.6 2.4 fusion.10
  167.0 2.7 convolution_convert_fusion
  170.3 2.4 fusion.7
  172.8 32.8 %all-gather.7.cloned.1.call-done = bf16[32,4,4096]{2,1,0:T(4,128)(2,1)} async-done(((bf16[1,4,4096]{2,1,0:T(4,128)(2,1)}), bf16[32,4,4096]{2,1,0:T(4,128)(2,1)}) %all-gather.7.cloned.1.call-update) | async-done | bytes 1048592 | tf_op jit(solution)/shard_map/all_gather | solution.py:293
  205.6 1.3 reshape.446
  208.8 136.7 %reduce-scatter.2.cloned.1.call-done = bf16[32,1024]{1,0:T(8,128)(2,1)} async-done(((bf16[1024,1024]{1,0:T(8,128)(2,1)}), bf16[32,1024]{1,0:T(8,128)(2,1)}) %reduce-scatter.2.cloned.1.call-update) | async-done | bytes 65552 | tf_op jit(solution)/shard_map/reduce_scatter | solution.py:291
  345.6 1.4 fusion.84
  (88 shorter events, 12.5 us)
Async XLA Ops:
  7.2 4.0 %copy-start = (bf16[1,4,128,1024]{3,2,1,0:T(8,128)(2,1)S(1)}, bf16[1,4,128,1024]{3,2,1,0:T(8,128)(2,1)}, u32[]{:S(2)}) copy-start(bf16[1,4,128,1024]{3,2,1,0:T(8,128)(2,1)} %param.10) | copy-start | bytes 3145732
  7.2 76.5 %all-gather.5.cloned.1.call-start = ((), (), s32[]{:S(2)}) async-start(), calls=%async_computation.1 | async-start | bytes 6488064 | tf_op jit(solution)/shard_map/all_gather | solution.py:244
  8.9 196.7 %all-gather.7.cloned.1.call-start = ((), (), s32[]{:S(2)}) async-start(), calls=%async_computation.3 | async-start | bytes 1081344 | tf_op jit(solution)/shard_map/all_gather | solution.py:293
  12.2 1.8 copy-start.9
  92.2 1.3 copy-start.4
  98.1 2.2 copy-start.2
  98.2 2.2 copy-start.3
  100.6 3.0 copy-start.5
  100.6 3.0 copy-start.6
  100.6 3.2 copy-start.8
  103.8 46.5 %copy-start.7 = (f32[4]{0:T(128)}, f32[4]{0:T(128)S(1)}, u32[]{:S(2)}) copy-start(f32[4]{0:T(128)S(1)} %multiply_reduce_fusion.6) | copy-start | bytes 52
  151.4 194.1 %reduce-scatter.2.cloned.1.call-start = ((), (), s32[]{:S(2)}) async-start(), calls=%async_computation.2 | async-start | bytes 2162688 | tf_op jit(solution)/shard_map/reduce_scatter | solution.py:291
  162.5 2.0 copy-start.1
Sparse Core Ops, SparseCore 0:
  11.6 72.0 all-gather.4
  151.5 54.0 all-gather.6
  207.9 137.6 reduce-scatter.1

commit v2 on v1

--- a/solution.py
+++ b/solution.py
@@ -1,10 +1,12 @@
 import jax
 import jax.numpy as jnp
 from jax import lax
+from jax.experimental import pallas as pl
+from jax.experimental.pallas import tpu as pltpu
 from jax.sharding import PartitionSpec as P
 
 HEAD_WIDTH = 128
-
+MESH_ID = pl.DeviceIdType.MESH
 
 EPSILON = 1e-06
 ROPE_BASE = 1000000.0
@@ -224,6 +226,337 @@
     return (grad_input.astype(jnp.bfloat16), last_rows, grad_kv)
 
 
+class Place:
+    def __init__(self):
+        self.pb_count = lax.axis_size("pb")
+        self.neg_count = lax.axis_size("neg")
+        self.line_count = self.neg_count // 2
+        self.pb = lax.axis_index("pb")
+        neg = lax.axis_index("neg")
+        self.line = neg // 2
+        self.core = neg % 2
+        self.partner = 1 - self.core
+
+    def slot(self, pb, line, core):
+        return pb * self.neg_count + line * 2 + core
+
+    def line_peer(self, step):
+        return lax.rem(self.line + step, self.line_count)
+
+    def pb_peer(self, step):
+        return lax.rem(self.pb + step, self.pb_count)
+
+    def to_line(self, line):
+        return (self.pb, line * 2 + self.core)
+
+    def to_pb(self, pb):
+        return (pb, self.line * 2 + self.core)
+
+    def to_partner(self):
+        return (self.pb, self.line * 2 + self.partner)
+
+    def greet(self):
+        barrier = pltpu.get_barrier_semaphore()
+        targets = [self.to_line(self.line_peer(k)) for k in range(1, self.line_count)]
+        targets += [self.to_pb(self.pb_peer(k)) for k in range(1, self.pb_count)]
+        targets += [self.to_partner()]
+        for target in targets:
+            pl.semaphore_signal(barrier, inc=1, device_id=target, device_id_type=MESH_ID)
+        pl.semaphore_wait(barrier, len(targets))
+
+
+def remote(src, dst, send_sem, recv_sem, target):
+    return pltpu.make_async_remote_copy(
+        src_ref=src,
+        dst_ref=dst,
+        send_sem=send_sem,
+        recv_sem=recv_sem,
+        device_id=target,
+        device_id_type=MESH_ID,
+    )
+
+
+def gather_sems(pb_count, neg_count):
+    line_count = neg_count // 2
+    return [
+        pltpu.SemaphoreType.DMA((line_count,)),
+        pltpu.SemaphoreType.DMA((line_count,)),
+        pltpu.SemaphoreType.DMA((pb_count, line_count)),
+        pltpu.SemaphoreType.DMA((pb_count, line_count)),
+        pltpu.SemaphoreType.DMA((pb_count, line_count)),
+        pltpu.SemaphoreType.DMA((pb_count, line_count)),
+        pltpu.SemaphoreType.DMA,
+    ]
+
+
+class Gather:
+    def __init__(self, place, own, full, sems):
+        self.place, self.own, self.full = place, own, full
+        self.line_send, self.line_recv, self.pb_send, self.pb_recv = sems[:4]
+        self.core_send, self.core_recv, self.local_sem = sems[4:]
+        self.sent = []
+
+    def rows(self, pb, line, core):
+        size = self.own.shape[0]
+        start = self.place.slot(pb, line, core) * size
+        return self.full.at[pl.ds(pl.multiple_of(start, size), size)]
+
+    def send(self, src, dst, send_sem, recv_sem, target):
+        copy = remote(src, dst, send_sem, recv_sem, target)
+        copy.start()
+        self.sent.append(copy)
+
+    def spread(self, src, line):
+        at = self.place
+        dst = self.rows(at.pb, line, at.core)
+        for k in range(1, at.pb_count):
+            self.send(
+                src, dst, self.pb_send.at[k, line], self.pb_recv.at[at.pb, line], at.to_pb(at.pb_peer(k))
+            )
+        self.pass_on(src, at.pb, line)
+
+    def pass_on(self, src, pb, line):
+        at = self.place
+        dst = self.rows(pb, line, at.core)
+        self.send(src, dst, self.core_send.at[pb, line], self.core_recv.at[pb, line], at.to_partner())
+
+    def arrive(self, block, recv_sem):
+        remote(block, block, self.local_sem, recv_sem, self.place.to_partner()).wait_recv()
+
+    def start(self):
+        at = self.place
+        mine = self.rows(at.pb, at.line, at.core)
+        self.local = pltpu.make_async_copy(self.own, mine, self.local_sem)
+        self.local.start()
+        for k in range(1, at.line_count):
+            line = at.line_peer(k)
+            self.send(
+                self.own, mine, self.line_send.at[k], self.line_recv.at[at.line], at.to_line(line)
+            )
+        self.spread(self.own, at.line)
+
+    def middle(self):
+        at = self.place
+        for k in range(1, at.line_count):
+            line = at.line_peer(k)
+            block = self.rows(at.pb, line, at.core)
+            self.arrive(block, self.line_recv.at[line])
+            self.spread(block, line)
+
+    def finish(self):
+        at = self.place
+        for step in range(at.line_count):
+            line = at.line_peer(step)
+            for k in range(1, at.pb_count):
+                pb = at.pb_peer(k)
+                block = self.rows(pb, line, at.core)
+                self.arrive(block, self.pb_recv.at[pb, line])
+                self.pass_on(block, pb, line)
+        for pb in range(at.pb_count):
+            for line in range(at.line_count):
+                self.arrive(self.rows(pb, line, at.partner), self.core_recv.at[pb, line])
+        for copy in self.sent:
+            copy.wait_send()
+        self.local.wait()
+
+
+def gather_kernel(own, full, *sems):
+    place = Place()
+    place.greet()
+    gather = Gather(place, own, full, sems)
+    gather.start()
+    gather.middle()
+    gather.finish()
+
+
+VMEM_SPEC = pl.BlockSpec(memory_space=pltpu.VMEM)
+
+
+def gather_weights(packed, pb_count, neg_count):
+    return pl.pallas_call(
+        gather_kernel,
+        out_shape=jax.ShapeDtypeStruct(
+            (packed.shape[0] * pb_count * neg_count, packed.shape[1]), packed.dtype
+        ),
+        in_specs=[VMEM_SPEC],
+        out_specs=VMEM_SPEC,
+        scratch_shapes=gather_sems(pb_count, neg_count),
+        compiler_params=pltpu.CompilerParams(
+            collective_id=0, has_side_effects=True, vmem_limit_bytes=32 * 2**20
+        ),
+    )(packed)
+
+
+def listing_kernel(own, full, send, recv, local_sem):
+    at = Place()
+    barrier = pltpu.get_barrier_semaphore()
+    neg = lax.axis_index("neg")
+    peers = [lax.rem(neg + k, at.neg_count) for k in range(1, at.neg_count)]
+    for peer in peers:
+        pl.semaphore_signal(barrier, inc=1, device_id=(at.pb, peer), device_id_type=MESH_ID)
+    pl.semaphore_wait(barrier, len(peers))
+    copies = []
+    local = pltpu.make_async_copy(own, full.at[neg], local_sem)
+    local.start()
+    for k, peer in enumerate(peers):
+        copy = remote(own, full.at[neg], send.at[k], recv.at[neg], (at.pb, peer))
+        copy.start()
+        copies.append(copy)
+    local.wait()
+    for peer in peers:
+        block = full.at[peer]
+        remote(block, block, local_sem, recv.at[peer], (at.pb, peer)).wait_recv()
+    for copy in copies:
+        copy.wait_send()
+
+
+def exchange_listing(own, neg_count):
+    return pl.pallas_call(
+        listing_kernel,
+        out_shape=jax.ShapeDtypeStruct((neg_count,) + own.shape, own.dtype),
+        in_specs=[VMEM_SPEC],
+        out_specs=VMEM_SPEC,
+        scratch_shapes=[
+            pltpu.SemaphoreType.DMA((neg_count,)),
+            pltpu.SemaphoreType.DMA((neg_count,)),
+            pltpu.SemaphoreType.DMA,
+        ],
+        compiler_params=pltpu.CompilerParams(collective_id=1, has_side_effects=True),
+    )(own)
+
+
+def reduce_kernel(
+    partial,
+    last_rows,
+    loss_row,
+    reduced,
+    all_rows,
+    all_losses,
+    from_core,
+    paired,
+    from_pb,
+    summed,
+    from_line,
+    core_send,
+    core_recv,
+    pb_send,
+    pb_recv,
+    line_send,
+    line_recv,
+    loss_send,
+    loss_recv,
+    loss_local,
+    *sems,
+):
+    at = Place()
+    at.greet()
+    gather = Gather(at, last_rows, all_rows, sems)
+    copies = []
+
+    def send(src, dst, send_sem, recv_sem, target):
+        copy = remote(src, dst, send_sem, recv_sem, target)
+        copy.start()
+        copies.append(copy)
+
+    def arrive(block, recv_sem):
+        remote(block, block, loss_local, recv_sem, at.to_partner()).wait_recv()
+
+    for k in range(1, at.pb_count + 1):
+        pb = at.pb_peer(k % at.pb_count)
+        send(
+            partial.at[pb, :, at.partner],
+            from_core.at[pb],
+            core_send.at[pb],
+            core_recv.at[pb],
+            at.to_partner(),
+        )
+    gather.start()
+    local = pltpu.make_async_copy(loss_row, all_losses.at[at.pb], loss_local)
+    local.start()
+    for k in range(1, at.pb_count):
+        send(
+            loss_row, all_losses.at[at.pb], loss_send.at[k], loss_recv.at[at.pb], at.to_pb(at.pb_peer(k))
+        )
+    for k in range(1, at.pb_count + 1):
+        pb = at.pb_peer(k % at.pb_count)
+        arrive(from_core.at[pb], core_recv.at[pb])
+        both = partial[pb, :, at.core].astype(jnp.float32) + from_core[pb].astype(jnp.float32)
+        paired[pb] = both.astype(jnp.bfloat16)
+        if k < at.pb_count:
+            send(
+                paired.at[pb], from_pb.at[at.pb], pb_send.at[k], pb_recv.at[at.pb], at.to_pb(pb)
+            )
+    gather.middle()
+    for k in range(1, at.pb_count):
+        pb = at.pb_peer(k)
+        arrive(from_pb.at[pb], pb_recv.at[pb])
+    for step in range(1, at.line_count + 1):
+        line = at.line_peer(step % at.line_count)
+        total = paired[at.pb, line].astype(jnp.float32)
+        for k in range(1, at.pb_count):
+            total = total + from_pb[at.pb_peer(k), line].astype(jnp.float32)
+        if step < at.line_count:
+            summed[line] = total.astype(jnp.bfloat16)
+            send(
+                summed.at[line],
+                from_line.at[at.line],
+                line_send.at[line],
+                line_recv.at[at.line],
+                at.to_line(line),
+            )
+    for step in range(1, at.line_count):
+        line = at.line_peer(step)
+        arrive(from_line.at[line], line_recv.at[line])
+        total = total + from_line[line].astype(jnp.float32)
+    reduced[...] = total
+    gather.finish()
+    local.wait()
+    for k in range(1, at.pb_count):
+        pb = at.pb_peer(k)
+        arrive(all_losses.at[pb], loss_recv.at[pb])
+    for copy in copies:
+        copy.wait_send()
+
+
+def reduce_gradients(grad_kv, last_rows, loss_row, pb_count, neg_count):
+    line_count = neg_count // 2
+    share = grad_kv.shape[0] // (pb_count * neg_count)
+    width = grad_kv.shape[1]
+    partial = grad_kv.reshape(pb_count, line_count, 2, share, width)
+    block = (pb_count, line_count, share, width)
+    dma = pltpu.SemaphoreType.DMA
+    return pl.pallas_call(
+        reduce_kernel,
+        out_shape=(
+            jax.ShapeDtypeStruct((share, width), jnp.float32),
+            jax.ShapeDtypeStruct((last_rows.shape[0] * pb_count * neg_count, last_rows.shape[1]), last_rows.dtype),
+            jax.ShapeDtypeStruct((pb_count,) + loss_row.shape, loss_row.dtype),
+        ),
+        in_specs=[VMEM_SPEC] * 3,
+        out_specs=(VMEM_SPEC,) * 3,
+        scratch_shapes=[
+            pltpu.VMEM(block, jnp.bfloat16),
+            pltpu.VMEM(block, jnp.bfloat16),
+            pltpu.VMEM(block, jnp.bfloat16),
+            pltpu.VMEM(block[1:], jnp.bfloat16),
+            pltpu.VMEM(block[1:], jnp.bfloat16),
+            dma((pb_count,)),
+            dma((pb_count,)),
+            dma((pb_count,)),
+            dma((pb_count,)),
+            dma((line_count,)),
+            dma((line_count,)),
+            dma((pb_count,)),
+            dma((pb_count,)),
+            dma,
+        ]
+        + gather_sems(pb_count, neg_count),
+        compiler_params=pltpu.CompilerParams(
+            collective_id=2, has_side_effects=True, vmem_limit_bytes=40 * 2**20
+        ),
+    )(partial, last_rows, loss_row)
+
+
 def shards(
     hidden,
     lengths,
@@ -241,7 +574,12 @@
     kv_width = key_matrix.shape[1]
     head_width = out_weight.shape[0]
     packed = jnp.concatenate([query_weight, key_matrix, value_matrix, out_weight.T], axis=1)
-    everything = lax.all_gather(packed, both, axis=0, tiled=True)
+    pb_count, neg_count = lax.axis_size("pb"), lax.axis_size("neg")
+    own_kernels = packed.shape[0] % 16 == 0 and neg_count % 2 == 0
+    if own_kernels:
+        everything = gather_weights(packed, pb_count, neg_count)
+    else:
+        everything = lax.all_gather(packed, both, axis=0, tiled=True)
     full_query = everything[:, :width]
     full_key = everything[:, width : width + kv_width]
     full_value = everything[:, width + kv_width : width + 2 * kv_width]
@@ -259,21 +597,22 @@
     )
     pair_count = scores_here.shape[0]
     row = lax.axis_index("pb")
-    listed = lax.all_gather(jnp.concatenate([scores_here, teacher[0]])[None], both, axis=0, tiled=True)
-    listed = listed.reshape(lax.axis_size("pb"), -1, 2, pair_count)
-    all_scores = listed[:, :, 0].reshape(listed.shape[0], -1)
-    all_scaled = listed[:, :, 1].reshape(listed.shape[0], -1) / TEACHER_TEMP
-    total_s = jnp.sum(jnp.exp(all_scores), axis=1, keepdims=True)
+    listing = jnp.concatenate([scores_here, teacher[0]])[None]
+    if own_kernels:
+        lanes = jnp.pad(listing, ((0, 0), (0, HEAD_WIDTH - 2 * pair_count)))
+        listed = exchange_listing(lanes, neg_count)[:, 0, : 2 * pair_count]
+    else:
+        listed = lax.all_gather(listing, "neg", axis=0, tiled=True)
+    all_scores = listed[:, :pair_count]
+    all_scaled = listed[:, pair_count:] / TEACHER_TEMP
+    my_total_s = jnp.sum(jnp.exp(all_scores))
     expo_t = jnp.exp(all_scaled)
-    total_t = jnp.sum(expo_t, axis=1, keepdims=True)
-    loss_value = jnp.sum(
+    my_total_t = jnp.sum(expo_t)
+    loss_here = jnp.sum(
         expo_t
-        / total_t
-        * (all_scaled - jnp.log(total_t) - (all_scores - jnp.log(total_s)))
-    )
-    mine = (jnp.arange(listed.shape[0]) == row)[:, None]
-    my_total_s = jnp.sum(jnp.where(mine, total_s, 0.0))
-    my_total_t = jnp.sum(jnp.where(mine, total_t, 0.0))
+        / my_total_t
+        * (all_scaled - jnp.log(my_total_t) - (all_scores - jnp.log(my_total_s)))
+    )
     prob_s = jnp.exp(scores_here) / my_total_s
     prob_t = jnp.exp(teacher[0] / TEACHER_TEMP) / my_total_t
     grad_score = GRAD_SCALE * (prob_s - prob_t)
@@ -288,9 +627,20 @@
         full_value,
         full_out_t.T,
     )
-    reduced = lax.psum_scatter(grad_kv.astype(jnp.bfloat16), both, scatter_dimension=0, tiled=True)
-    reduced = reduced.astype(jnp.float32)
-    rows = lax.all_gather(last_rows, both, axis=0, tiled=True)
+    grad_kv = grad_kv.astype(jnp.bfloat16)
+    if own_kernels:
+        spaced = jnp.pad(last_rows.reshape(pair_count * 4, -1), ((0, -pair_count * 4 % 16), (0, 0)))
+        reduced, rows, losses = reduce_gradients(
+            grad_kv, spaced, jnp.full((1, HEAD_WIDTH), loss_here), pb_count, neg_count
+        )
+        rows = rows.reshape(-1, spaced.shape[0], spaced.shape[1])[:, : pair_count * 4]
+        rows = rows.reshape(pb_count * neg_count * pair_count, -1)
+        loss_value = jnp.sum(losses[:, 0, 0])
+    else:
+        reduced = lax.psum_scatter(grad_kv, both, scatter_dimension=0, tiled=True)
+        reduced = reduced.astype(jnp.float32)
+        rows = lax.all_gather(last_rows, both, axis=0, tiled=True)
+        loss_value = lax.psum(loss_here, "pb")
     index = row * lax.axis_size("neg") + lax.axis_index("neg")
     share = query_weight.shape[0]
     model_width = share * lax.axis_size("pb") * lax.axis_size("neg")

time: 354 us -> 149 us (0.42)
  waiting for transfers between devices: 238 us -> 0 us
  Pallas kernels: 0 us -> 85.3 us
  blocking collectives: 39.2 us -> 0 us
  between operations: 14.2 us -> 2.38 us
    reduce_scatter x1 -> x0, waiting for transfers between devices: 137 us -> none  [shards(): lax.psum_scatter(grad_kv.astype(jnp.bfloat16), both, scatter_dimension=0,...]
    all_gather x2 -> x0, waiting for transfers between devices: 102 us -> none  [the longest x1 68.7 us: shards(): everything = lax.all_gather(packed, both, axis=0, tiled=True)]
    pallas_call x0 -> x3, Pallas kernels: none -> 85.3 us  [the longest x1 46.7 us: gather_weights(): pl.pallas_call(gather_kernel, out_shape=jax.ShapeDtypeStruct((packed.shap...]
    unnamed x1 -> x0, blocking collectives: 39.2 us -> none
  transfers between devices with their start and end apart: 3 -> 0, of which waited for: 3 -> 0; matrix products, arithmetic and copies ran while one was open for 9% -> 0% of each run, Pallas kernels for 0% -> 0%
where the time goes in v2:
time: 149 us; the launch traced here: 148 us
  Pallas kernels  85.3 us (57%)
  matrix products  23.6 us (16%)
  local copies, waits for them, and re-layouts  19.6 us (13%)
  other arithmetic  16.9 us (11%)
  between operations  2.38 us (2%)
    pallas_call x1, Pallas kernels, gather_weights(): pl.pallas_call(gather_kernel, out_shape=jax.ShapeDtypeStruct((packed.shap...  46.7 us
    pallas_call x1, Pallas kernels, reduce_gradients(): pl.pallas_call(reduce_kernel, out_shape=(jax.ShapeDtypeStruct((share, wid...  27 us
    pallas_call x1, Pallas kernels, exchange_listing(): pl.pallas_call(listing_kernel, out_shape=jax.ShapeDtypeStruct((neg_count,...  11.5 us
    dot_general x2, local copies, waits for them, and re-layouts, forward_pairs(): jnp.dot(normed_last, query_weight, preferred_element_type=jnp.float32)  4.46 us
    convert_element_type x1, other arithmetic, backward_pairs(): return (grad_input.astype(jnp.bfloat16), last_rows, grad_kv)  4.06 us
    dot_general x1, matrix products, backward_pairs(): jnp.dot(grad_v_cast, value_matrix.T, preferred_element_type=jnp.float32)  3.68 us
    dot_general x2, local copies, waits for them, and re-layouts, forward_pairs(): jnp.dot(flat_rows, key_matrix, preferred_element_type=jnp.float32)  3.18 us

profile of v2, /device:TPU:0, one launch (start us, length us, event | category | flops | bytes accessed | tf_op | source)
XLA Modules:
  0.0 147.8 jit_solution(8616312452686588954)
XLA Ops:
  0.6 0.9 pad_maximum_fusion.own
  1.6 46.7 %shard_map.153 = bf16[1024,3072]{1,0:T(8,128)(2,1)S(1)} custom-call(bf16[32,3072]{1,0:T(8,128)(2,1)S(1)} %pad_maximum_fusion.own), custom_call_target="tpu_custom_call" | custom-call | tf_op jit(solution)/shard_map/pallas_call | solution.py:376
  48.3 2.7 %copy-done = bf16[1024,3072]{1,0:T(8,128)(2,1)} copy-done((bf16[1024,3072]{1,0:T(8,128)(2,1)}, bf16[1024,3072]{1,0:T(8,128)(2,1)S(1)}, u32[]{:S(2)}) %copy-start) | copy-done | bytes 6291480
  50.9 1.5 %slice_bitcast_fusion = bf16[1024,1024]{0,1:T(8,128)(2,1)} fusion(bf16[1024,3072]{1,0:T(8,128)(2,1)S(1)} %shard_map.153), kind=kLoop, calls=%fused_computation.29 | loop fusion | bytes 4194304 | tf_op jit(solution)/shard_map/dot_general | solution.py:64
  52.4 2.9 %copy.38 = bf16[1024,1024]{1,0:T(8,128)(2,1)S(1)} copy(bf16[1024,1024]{0,1:T(8,128)(2,1)} %slice_bitcast_fusion) | data formatting | bytes 4194304 | tf_op jit(solution)/shard_map/dot_general | solution.py:64
  55.7 1.3 multiply_convert_fusion
  57.0 1.4 gather_fusion.1
  58.5 0.7 multiply_reduce_fusion.8
  60.4 2.7 %slice_bitcast_fusion.2 = (bf16[512,1024]{0,1:T(8,128)(2,1)S(1)}, bf16[512,1024]{0,1:T(8,128)(2,1)}) fusion(bf16[1024,3072]{1,0:T(8,128)(2,1)} %copy-done), kind=kLoop, calls=%fused_computation.57 | loop fusion | bytes 4194304 | tf_op jit(solution)/shard_map/dot_general | solution.py:54
  63.6 0.8 multiply_reduce_fusion.2
  65.4 2.3 %copy.40 = bf16[512,1024]{1,0:T(8,128)(2,1)} copy(bf16[512,1024]{0,1:T(8,128)(2,1)} %get-tuple-element.18) | data formatting | bytes 2097152 | tf_op jit(solution)/shard_map/dot_general | solution.py:57
  67.7 2.0 %convolution_convert_fusion.2 = bf16[4,128,4,128]{3,1,2,0:T(8,128)(2,1)S(1)} fusion(bf16[4,128,1024,1]{2,1,0,3:T(8,128)(2,1)} %bitcast.139, bf16[1,4,128,1024]{3,2,1,0:T(8,128)(2,1)S(1)} %copy-done.1, f32[1024]{0:T(1024)S(1)} %copy-done.2, f32[4,128]{1,0:T(4,128)S(1)} %get-tuple-element.36), kind=kOutput, calls=%fused_computation.33 | convolution fusion | flops 539230208 | bytes 2627584 | tf_op jit(solution)/shard_map/dot_general | solution.py:57
  70.1 1.6 %convert_bitcast_fusion = f32[4,128,1024]{2,1,0:T(8,128)} fusion(bf16[1,4,128,1024]{3,2,1,0:T(8,128)(2,1)S(1)} %copy-done.1), kind=kLoop, calls=%fused_computation.9 | loop fusion | flops 524288 | bytes 3145728 | tf_op jit(solution)/shard_map/convert_element_type | solution.py:50
  71.7 1.4 gather_fusion
  73.1 2.4 %multiply_reduce_fusion.7 = (f32[4]{0:T(128)S(1)}, f32[4,1024]{1,0:T(4,128)S(1)}) fusion(bf16[4,1024]{1,0:T(4,128)(2,1)S(1)} %reshape.387, bf16[1024,3072]{1,0:T(8,128)(2,1)} %copy-done, f32[4,1024]{1,0:T(4,128)S(1)} %gather_fusion, pred[4]{0:T(512)(128)(4,1)S(1)} %compare_and_fusion), kind=kOutput, calls=%fused_computation.95 | convolution fusion | flops 8404988 | bytes 2138132 | tf_op jit(solution)/shard_map/dot_general | solution.py:93
  76.3 11.5 %shard_map.154 = f32[8,1,128]{2,1,0:T(1,128)} custom-call(f32[1,128]{1,0:T(1,128)} %pad.4.own), custom_call_target="tpu_custom_call" | custom-call | tf_op jit(solution)/shard_map/pallas_call | solution.py:414
  87.8 1.4 exponential_reduce_fusion
  90.6 2.1 %multiply_reduce_fusion.9 = f32[]{:T(128)} fusion(f32[8,8]{1,0:T(8,128)} %bitcast.141, f32[]{:T(128)S(6)} %log.7, f32[]{:T(128)S(6)} %log.6, f32[]{:T(128)} %get-tuple-element.14), kind=kLoop, calls=%fused_computation.109 | loop fusion | flops 223 | bytes 272 | tf_op jit(solution)/shard_map/reduce_sum | solution.py:611
  92.7 0.6 broadcast_in_dim.45.loss_row
  93.4 1.3 fusion.71
  95.0 2.0 %fusion.26 = bf16[4,1024]{1,0:T(4,128)(2,1)S(1)} fusion(bf16[4,1024]{1,0:T(4,128)(2,1)S(1)} %get-tuple-element.15, bf16[1024,3072]{1,0:T(8,128)(2,1)} %copy-done), kind=kOutput, calls=%fused_computation.40 | convolution fusion | flops 8392704 | bytes 2113536 | tf_op jit(solution)/shard_map/dot_general | solution.py:167
  101.0 2.0 %fusion.36 = f32[512,1024]{1,0:T(8,128)S(1)} fusion(bf16[1024,3072]{1,0:T(8,128)(2,1)} %copy-done, bf16[64,8,4,128]{3,2,1,0:T(4,128)(2,1)S(1)} %bitcast.137), kind=kOutput, calls=%fused_computation.55 | convolution fusion | flops 536870912 | bytes 3670016 | tf_op jit(solution)/shard_map/dot_general | solution.py:213
  103.0 2.2 %fusion.18 = f32[4,1024]{1,0:T(4,128)S(1)} fusion(bf16[4,1024]{1,0:T(4,128)(2,1)S(1)} %fusion.51, bf16[1024,3072]{1,0:T(8,128)(2,1)} %copy-done), kind=kOutput, calls=%fused_computation.27 | convolution fusion | flops 8388608 | bytes 2121728 | tf_op jit(solution)/shard_map/dot_general | solution.py:218
  105.2 3.7 %fusion.3 = (f32[512]{0:T(512)S(1)}, bf16[512,1024]{1,0:T(8,128)(2,1)S(1)}, f32[512,1024]{1,0:T(8,128)}) fusion(bf16[1,4,128,1024]{3,2,1,0:T(8,128)(2,1)S(1)} %copy-done.1, f32[4,1024]{1,0:T(4,128)S(1)} %fusion.18, f32[512]{0:T(512)S(1)} %get-tuple-element.38, f32[1024]{0:T(1024)S(1)} %copy-done.2, f32[512]{0:T(512)S(1)} %get-tuple-element.35, ...), kind=kOutput, calls=%fused_computation.6 | convolution fusion | flops 542113280 | bytes 7890944 | tf_op jit(solution)/shard_map/dot_general | solution.py:214
  108.9 1.3 convolution_convert_fusion
  110.2 27.0 %shard_map.155 = (f32[32,1024]{1,0:T(8,128)S(1)}, bf16[512,1024]{1,0:T(8,128)(2,1)S(1)}, f32[4,1,128]{2,1,0:T(1,128)S(1)}) custom-call(bf16[4,4,2,32,1024]{4,3,2,1,0:T(8,128)(2,1)S(1)} %bitcast.131, bf16[16,1024]{1,0:T(8,128)(2,1)S(1)} %reshape.391.last_rows, f32[1,128]{1,0:T(1,128)S(1)} %broadcast_in_dim.45.loss_row), custom_call_target="tpu_custom_call" | custom-call | tf_op jit(solution)/shard_map/pallas_call | solution.py:528
  137.2 1.5 reshape_reshape.3
  138.7 1.9 %fusion.41 = f32[1024,32]{0,1:T(8,128)} fusion(bf16[128,4096]{1,0:T(8,128)(2,1)} %reshape_reshape.3, s32[]{:T(128)S(6)} %select_n.67), kind=kOutput, calls=%fused_computation.65 | convolution fusion | flops 8388608 | bytes 425988 | tf_op jit(solution)/shard_map/dot_general | solution.py:654
  140.6 1.9 %fusion.43 = f32[32,1024]{1,0:T(8,128)} fusion(bf16[128,4096]{1,0:T(8,128)(2,1)} %reshape_reshape.3, s32[]{:T(128)S(6)} %select_n.66), kind=kOutput, calls=%fused_computation.67 | convolution fusion | flops 8388608 | bytes 425988 | tf_op jit(solution)/shard_map/dot_general | solution.py:653
  142.5 4.1 %fusion.11 = bf16[1,4,128,1024]{3,2,1,0:T(8,128)(2,1)} fusion(bf16[1,4,128,1024]{3,2,1,0:T(8,128)(2,1)S(1)} %copy-done.1, f32[1,4,128,1024]{3,2,1,0:T(8,128)} %bitcast.132, f32[4,1024]{1,0:T(4,128)S(1)} %get-tuple-element.16, f32[4,128]{1,0:T(4,128)S(1)} %multiply_bitcast_fusion, f32[4,1024]{1,0:T(4,128)S(1)} %fusion.18, f32[4,128]{1,0:T(4,128)S(1)} %get-tuple-element.37, ...), kind=kLoop, calls=%fused_computation.17 | loop fusion | flops 6815744 | bytes 4237312 | tf_op jit(solution)/shard_map/convert_element_type | solution.py:226
  146.6 0.7 fusion.82
  147.2 0.6 slice_reduce_fusion
  (73 shorter events, 8.4 us)
Async XLA Ops:
  48.3 2.7 %copy-start = (bf16[1024,3072]{1,0:T(8,128)(2,1)}, bf16[1024,3072]{1,0:T(8,128)(2,1)S(1)}, u32[]{:S(2)}) copy-start(bf16[1024,3072]{1,0:T(8,128)(2,1)S(1)} %shard_map.153) | copy-start | bytes 18874372
  52.4 3.0 %copy-start.1 = (bf16[1,4,128,1024]{3,2,1,0:T(8,128)(2,1)S(1)}, bf16[1,4,128,1024]{3,2,1,0:T(8,128)(2,1)}, u32[]{:S(2)}) copy-start(bf16[1,4,128,1024]{3,2,1,0:T(8,128)(2,1)} %param.10) | copy-start | bytes 3145732
  52.4 3.3 %copy-start.2 = (f32[1024]{0:T(1024)S(1)}, f32[1024]{0:T(1024)}, u32[]{:S(2)}) copy-start(f32[1024]{0:T(1024)} %param.13) | copy-start | bytes 12292
  55.4 1.6 %copy-start.7 = (s32[1,4]{1,0:T(1,128)S(1)}, s32[1,4]{1,0:T(1,128)}, u32[]{:S(2)}) copy-start(s32[1,4]{1,0:T(1,128)} %param.11) | copy-start | bytes 52
  70.0 5.4 %copy-start.3 = (f32[1024]{0:T(1024)S(1)}, f32[1024]{0:T(1024)}, u32[]{:S(2)}) copy-start(f32[1024]{0:T(1024)} %param.15) | copy-start | bytes 12292
  70.0 5.4 %copy-start.4 = (f32[1024]{0:T(1024)S(1)}, f32[1024]{0:T(1024)}, u32[]{:S(2)}) copy-start(f32[1024]{0:T(1024)} %param.14) | copy-start | bytes 12292
  70.1 5.6 %copy-start.6 = (f32[1,4]{1,0:T(1,128)S(1)}, f32[1,4]{1,0:T(1,128)}, u32[]{:S(2)}) copy-start(f32[1,4]{1,0:T(1,128)} %param.12) | copy-start | bytes 52
  75.7 23.4 %copy-start.5 = (f32[4]{0:T(128)}, f32[4]{0:T(128)S(1)}, u32[]{:S(2)}) copy-start(f32[4]{0:T(128)S(1)} %multiply_reduce_fusion.6) | copy-start | bytes 52

commit v3 on v2

--- a/solution.py
+++ b/solution.py
@@ -1,3 +1,5 @@
+import functools
+
 import jax
 import jax.numpy as jnp
 from jax import lax
@@ -281,8 +283,10 @@
     return [
         pltpu.SemaphoreType.DMA((line_count,)),
         pltpu.SemaphoreType.DMA((line_count,)),
-        pltpu.SemaphoreType.DMA((pb_count, line_count)),
-        pltpu.SemaphoreType.DMA((pb_count, line_count)),
+        pltpu.SemaphoreType.DMA((2, line_count)),
+        pltpu.SemaphoreType.DMA((2, line_count)),
+        pltpu.SemaphoreType.DMA((2, line_count)),
+        pltpu.SemaphoreType.DMA((2, line_count)),
         pltpu.SemaphoreType.DMA((pb_count, line_count)),
         pltpu.SemaphoreType.DMA((pb_count, line_count)),
         pltpu.SemaphoreType.DMA,
@@ -293,8 +297,13 @@
     def __init__(self, place, own, full, sems):
         self.place, self.own, self.full = place, own, full
         self.line_send, self.line_recv, self.pb_send, self.pb_recv = sems[:4]
-        self.core_send, self.core_recv, self.local_sem = sems[4:]
+        self.half_send, self.half_recv = sems[4:6]
+        self.core_send, self.core_recv, self.local_sem = sems[6:]
         self.sent = []
+        across = place.pb + 1 - 2 * (place.pb % 2)
+        along = place.pb + 2 - 4 * (place.pb // 2)
+        self.near = (across, along)
+        self.corner = 3 - place.pb
 
     def rows(self, pb, line, core):
         size = self.own.shape[0]
@@ -309,9 +318,9 @@
     def spread(self, src, line):
         at = self.place
         dst = self.rows(at.pb, line, at.core)
-        for k in range(1, at.pb_count):
+        for side in range(2):
             self.send(
-                src, dst, self.pb_send.at[k, line], self.pb_recv.at[at.pb, line], at.to_pb(at.pb_peer(k))
+                src, dst, self.pb_send.at[side, line], self.pb_recv.at[side, line], at.to_pb(self.near[side])
             )
         self.pass_on(src, at.pb, line)
 
@@ -343,15 +352,35 @@
             self.arrive(block, self.line_recv.at[line])
             self.spread(block, line)
 
+    def half(self, block, side):
+        width = block.shape[1] // 2
+        return block.at[:, pl.ds(side * width, width)]
+
+    def relay(self):
+        at = self.place
+        for step in range(at.line_count):
+            line = at.line_peer(step)
+            for side in range(2):
+                block = self.rows(self.near[side], line, at.core)
+                self.arrive(block, self.pb_recv.at[side, line])
+                part = self.half(block, side)
+                self.send(
+                    part,
+                    part,
+                    self.half_send.at[side, line],
+                    self.half_recv.at[side, line],
+                    at.to_pb(self.near[1 - side]),
+                )
+                self.pass_on(block, self.near[side], line)
+
     def finish(self):
         at = self.place
         for step in range(at.line_count):
             line = at.line_peer(step)
-            for k in range(1, at.pb_count):
-                pb = at.pb_peer(k)
-                block = self.rows(pb, line, at.core)
-                self.arrive(block, self.pb_recv.at[pb, line])
-                self.pass_on(block, pb, line)
+            block = self.rows(self.corner, line, at.core)
+            for side in range(2):
+                self.arrive(self.half(block, side), self.half_recv.at[side, line])
+            self.pass_on(block, self.corner, line)
         for pb in range(at.pb_count):
             for line in range(at.line_count):
                 self.arrive(self.rows(pb, line, at.partner), self.core_recv.at[pb, line])
@@ -360,31 +389,42 @@
         self.local.wait()
 
 
-def gather_kernel(own, full, *sems):
+def gather_kernel(count, *refs):
     place = Place()
     place.greet()
-    gather = Gather(place, own, full, sems)
-    gather.start()
-    gather.middle()
-    gather.finish()
+    owns, fulls, sems = refs[:count], refs[count : 2 * count], refs[2 * count :]
+    each = len(sems) // count
+    gathers = [
+        Gather(place, owns[i], fulls[i], sems[i * each : (i + 1) * each]) for i in range(count)
+    ]
+    for gather in gathers:
+        gather.start()
+    for gather in gathers:
+        gather.middle()
+    for gather in gathers:
+        gather.relay()
+    for gather in gathers:
+        gather.finish()
 
 
 VMEM_SPEC = pl.BlockSpec(memory_space=pltpu.VMEM)
 
 
-def gather_weights(packed, pb_count, neg_count):
+def gather_weights(shares, pb_count, neg_count):
+    count = len(shares)
     return pl.pallas_call(
-        gather_kernel,
-        out_shape=jax.ShapeDtypeStruct(
-            (packed.shape[0] * pb_count * neg_count, packed.shape[1]), packed.dtype
+        functools.partial(gather_kernel, count),
+        out_shape=tuple(
+            jax.ShapeDtypeStruct((w.shape[0] * pb_count * neg_count, w.shape[1]), w.dtype)
+            for w in shares
         ),
-        in_specs=[VMEM_SPEC],
-        out_specs=VMEM_SPEC,
-        scratch_shapes=gather_sems(pb_count, neg_count),
+        in_specs=[VMEM_SPEC] * count,
+        out_specs=(VMEM_SPEC,) * count,
+        scratch_shapes=gather_sems(pb_count, neg_count) * count,
         compiler_params=pltpu.CompilerParams(
             collective_id=0, has_side_effects=True, vmem_limit_bytes=32 * 2**20
         ),
-    )(packed)
+    )(*shares)
 
 
 def listing_kernel(own, full, send, recv, local_sem):
@@ -487,6 +527,7 @@
                 paired.at[pb], from_pb.at[at.pb], pb_send.at[k], pb_recv.at[at.pb], at.to_pb(pb)
             )
     gather.middle()
+    gather.relay()
     for k in range(1, at.pb_count):
         pb = at.pb_peer(k)
         arrive(from_pb.at[pb], pb_recv.at[pb])
@@ -572,18 +613,19 @@
     both = ("pb", "neg")
     width = query_weight.shape[1]
     kv_width = key_matrix.shape[1]
-    head_width = out_weight.shape[0]
-    packed = jnp.concatenate([query_weight, key_matrix, value_matrix, out_weight.T], axis=1)
+    shares = (query_weight, key_matrix, value_matrix, out_weight.T)
     pb_count, neg_count = lax.axis_size("pb"), lax.axis_size("neg")
-    own_kernels = packed.shape[0] % 16 == 0 and neg_count % 2 == 0
+    even = all(w.shape[0] % 16 == 0 and w.shape[1] % (2 * HEAD_WIDTH) == 0 for w in shares)
+    own_kernels = even and pb_count == 4 and neg_count % 2 == 0
     if own_kernels:
-        everything = gather_weights(packed, pb_count, neg_count)
+        full_query, full_key, full_value, full_out_t = gather_weights(shares, pb_count, neg_count)
     else:
+        packed = jnp.concatenate(shares, axis=1)
         everything = lax.all_gather(packed, both, axis=0, tiled=True)
-    full_query = everything[:, :width]
-    full_key = everything[:, width : width + kv_width]
-    full_value = everything[:, width + kv_width : width + 2 * kv_width]
-    full_out_t = everything[:, width + 2 * kv_width :]
+        full_query = everything[:, :width]
+        full_key = everything[:, width : width + kv_width]
+        full_value = everything[:, width + kv_width : width + 2 * kv_width]
+        full_out_t = everything[:, width + 2 * kv_width :]
     scores_here, stored = forward_pairs(
         hidden[0],
         lengths[0],

time: 149 us -> 144 us (0.966)
  Pallas kernels: 85.3 us -> 76.4 us
  other arithmetic: 16.9 us -> 20 us
  matrix products: 23.6 us -> 26.2 us
  local copies, waits for them, and re-layouts: 19.6 us -> 17.8 us
    pallas_call x1, Pallas kernels: 46.7 us -> 39.4 us  [gather_weights(): pl.pallas_call(functools.partial(gather_kernel, count), out_shape=tuple((...]
    pallas_call x1, Pallas kernels: 11.5 us -> 8.01 us  [exchange_listing(): pl.pallas_call(listing_kernel, out_shape=jax.ShapeDtypeStruct((neg_count,...]
    dot_general x1, matrix products: 3.68 us -> 1.21 us  [backward_pairs(): jnp.dot(grad_v_cast, value_matrix.T, preferred_element_type=jnp.float32)]
    pallas_call x1, Pallas kernels: 27 us -> 29 us  [reduce_gradients(): pl.pallas_call(reduce_kernel, out_shape=(jax.ShapeDtypeStruct((share, wid...]
    dot_general x2 -> x1, local copies, waits for them, and re-layouts: 4.46 us -> 2.6 us  [forward_pairs(): jnp.dot(normed_last, query_weight, preferred_element_type=jnp.float32)]
    convert_element_type x1, local copies, waits for them, and re-layouts: 0.32 us -> 2.09 us  [backward_pairs(): grad_kproj.reshape(pair_count * seq_len, group_count * HEAD_WIDTH)]
    dot_general x1, matrix products: 0.72 us -> 2.36 us  [forward_pairs(): jnp.dot(normed_last, query_weight, preferred_element_type=jnp.float32)]
    dot_general x1, matrix products: 2.23 us -> 0.64 us  [backward_pairs(): jnp.dot(grad_q_cast, query_weight.T, preferred_element_type=jnp.float32)]
where the time goes in v3:
time: 144 us; the launch traced here: 143 us
  Pallas kernels  76.4 us (53%)
  matrix products  26.2 us (18%)
  other arithmetic  20 us (14%)
  local copies, waits for them, and re-layouts  17.8 us (12%)
  between operations  2.54 us (2%)
    pallas_call x1, Pallas kernels, gather_weights(): pl.pallas_call(functools.partial(gather_kernel, count), out_shape=tuple((...  39.4 us
    pallas_call x1, Pallas kernels, reduce_gradients(): pl.pallas_call(reduce_kernel, out_shape=(jax.ShapeDtypeStruct((share, wid...  29 us
    pallas_call x1, Pallas kernels, exchange_listing(): pl.pallas_call(listing_kernel, out_shape=jax.ShapeDtypeStruct((neg_count,...  8.01 us
    unnamed x65, local copies, waits for them, and re-layouts  3.94 us
    dot_general x1, matrix products, forward_pairs(): jnp.dot(flat_rows, value_matrix, preferred_element_type=jnp.float32)  3.11 us

profile of v3, /device:TPU:0, one launch (start us, length us, event | category | flops | bytes accessed | tf_op | source)
XLA Modules:
  0.0 142.9 jit_solution(320514408100106228)
XLA Ops:
  2.8 1.5 %multiply_reduce_fusion = f32[4,128]{1,0:T(4,128)S(1)} fusion(bf16[1,4,128,1024]{3,2,1,0:T(8,128)(2,1)} %param.10), kind=kLoop, calls=%fused_computation.21 | loop fusion | flops 1572352 | bytes 1050624 | tf_op jit(solution)/shard_map/reduce_sum | solution.py:53
  5.6 1.0 fusion.48
  6.6 1.0 fusion.49
  8.4 1.0 multiply_convert_fusion
  11.0 1.2 gather_fusion
  12.2 39.4 %shard_map.153 = (bf16[1024,1024]{1,0:T(8,128)(2,1)S(1)}, bf16[1024,512]{1,0:T(8,128)(2,1)S(1)}, bf16[1024,512]{1,0:T(8,128)(2,1)S(1)}, bf16[1024,1024]{1,0:T(8,128)(2,1)S(1)}) custom-call(bf16[32,1024]{1,0:T(8,128)(2,1)S(1)} %copy-done.3, bf16[32,512]{1,0:T(8,128)(2,1)S(1)} %copy-done.5, bf16[32,512]{1,0:T(8,128)(2,1)S(1)} %copy-done.6, ...), custom_call_target="tpu_custom_call" | custom-call | tf_op jit(solution)/shard_map/pallas_call | solution.py:415
  51.7 1.3 copy-done
  53.0 1.0 copy-done.1
  54.0 1.3 copy.40
  55.3 3.1 %convolution_convert_fusion.2 = bf16[4,128,4,128]{3,1,2,0:T(8,128)(2,1)} fusion(bf16[4,128,1024,1]{2,1,0,3:T(8,128)(2,1)} %bitcast.145, bf16[1,4,128,1024]{3,2,1,0:T(8,128)(2,1)} %param.10, f32[1024]{0:T(1024)S(1)} %copy-done.16, f32[4,128]{1,0:T(4,128)} %copy-done.20), kind=kOutput, calls=%fused_computation.26 | convolution fusion | flops 539230208 | bytes 2627584 | tf_op jit(solution)/shard_map/dot_general | solution.py:59
  58.4 2.3 %copy.39 = bf16[512,1024]{1,0:T(8,128)(2,1)} copy(bf16[512,1024]{0,1:T(8,128)(2,1)} %bitcast.135) | data formatting | bytes 2097152 | tf_op jit(solution)/shard_map/dot_general | solution.py:56
  60.7 2.4 %multiply_reduce_fusion.2 = (f32[4,128,4]{1,2,0:T(4,128)S(1)}, f32[4,128,4,128]{1,3,2,0:T(8,128)S(1)}) fusion(bf16[4,128,1024,1]{2,1,0,3:T(8,128)(2,1)} %bitcast.144, bf16[1,4,128,1024]{3,2,1,0:T(8,128)(2,1)} %param.10, f32[1024]{0:T(1024)S(1)} %copy-done.16, f32[4,128]{1,0:T(4,128)S(1)} %copy-done.21), kind=kOutput, calls=%fused_computation.45 | convolution fusion | flops 539490304 | bytes 3160064 | tf_op jit(solution)/shard_map/dot_general | solution.py:56
  64.0 1.0 fusion.19
  65.0 2.6 %copy.38 = bf16[1024,1024]{1,0:T(8,128)(2,1)} copy(bf16[1024,1024]{0,1:T(8,128)(2,1)S(1)} %bitcast.133) | data formatting | bytes 4194304 | tf_op jit(solution)/shard_map/dot_general | solution.py:66
  67.7 2.4 %multiply_reduce_fusion.8 = (f32[4,8]{0,1:T(8,128)S(1)}, f32[4,8,128]{2,0,1:T(4,128)S(1)}) fusion(bf16[8,128,1024]{2,1,0:T(8,128)(2,1)} %bitcast.139, bf16[4,1024]{1,0:T(4,128)(2,1)S(1)} %gather_fusion.1, pred[4]{0:T(512)(128)(4,1)S(1)} %copy-done.28), kind=kOutput, calls=%fused_computation.83 | convolution fusion | flops 8400864 | bytes 2121860 | tf_op jit(solution)/shard_map/dot_general | solution.py:66
  70.6 1.4 convolution_convert_fusion.4
  72.0 2.4 %multiply_reduce_fusion.7 = (f32[4]{0:T(128)S(1)}, f32[4,1024]{1,0:T(4,128)S(1)}) fusion(bf16[4,1024]{1,0:T(4,128)(2,1)S(1)} %reshape.387, bf16[1024,1024]{1,0:T(8,128)(2,1)} %copy-done, f32[4,1024]{1,0:T(4,128)S(1)} %copy-done.15, pred[4]{0:T(512)(128)(4,1)S(1)} %copy-done.28), kind=kOutput, calls=%fused_computation.82 | convolution fusion | flops 8404988 | bytes 2138132 | tf_op jit(solution)/shard_map/dot_general | solution.py:95
  75.2 8.0 %shard_map.154 = f32[8,1,128]{2,1,0:T(1,128)} custom-call(f32[1,128]{1,0:T(1,128)} %pad.4.own), custom_call_target="tpu_custom_call" | custom-call | tf_op jit(solution)/shard_map/pallas_call | solution.py:454
  83.2 1.4 %exponential_reduce_fusion = (f32[]{:T(128)}, f32[]{:T(128)}) fusion(f32[8,8]{1,0:T(8,128)} %bitcast.146), kind=kLoop, calls=%fused_computation.98 | loop fusion | flops 94 | bytes 264 | tf_op jit(solution)/shard_map/reduce_sum | solution.py:650
  86.0 2.1 %multiply_reduce_fusion.9 = f32[]{:T(128)} fusion(f32[8,8]{1,0:T(8,128)} %bitcast.147, f32[]{:T(128)S(6)} %log.7, f32[]{:T(128)S(6)} %log.6, f32[]{:T(128)} %get-tuple-element.22), kind=kLoop, calls=%fused_computation.96 | loop fusion | flops 223 | bytes 272 | tf_op jit(solution)/shard_map/reduce_sum | solution.py:653
  88.1 1.3 fusion.56
  90.4 2.0 %convolution_convert_fusion.3 = bf16[4,1024]{1,0:T(4,128)(2,1)S(1)} fusion(bf16[4,1024]{1,0:T(4,128)(2,1)S(1)} %get-tuple-element.23, bf16[1024,1024]{1,0:T(8,128)(2,1)} %copy-done), kind=kOutput, calls=%fused_computation.33 | convolution fusion | flops 8392704 | bytes 2113536 | tf_op jit(solution)/shard_map/dot_general | solution.py:169
  92.4 1.4 fusion.70
  94.1 1.4 convolution_multiply_fusion
  97.1 1.1 copy.32
  99.7 1.1 multiply_convert_fusion.1
  100.9 2.1 %copy.31 = bf16[4,128,4,128]{3,2,1,0:T(4,128)(2,1)} copy(bf16[4,128,4,128]{1,3,2,0:T(8,128)(2,1)} %multiply_convert_fusion.1) | data formatting | bytes 1048576 | tf_op jit(solution)/shard_map/convert_element_type | solution.py:202
  103.0 1.9 %fusion.65 = f32[512,1024]{1,0:T(8,128)S(1)} fusion(bf16[1024,512]{1,0:T(8,128)(2,1)S(1)} %copy-done.2, bf16[64,8,4,128]{3,2,1,0:T(4,128)(2,1)} %bitcast.142), kind=kOutput, calls=%fused_computation.138 | convolution fusion | flops 536870912 | bytes 3670016 | tf_op jit(solution)/shard_map/dot_general | solution.py:215
  104.9 1.2 fusion.3
  106.2 2.5 %fusion.11 = bf16[1,4,128,1024]{3,2,1,0:T(8,128)(2,1)} fusion(bf16[1,4,128,1024]{3,2,1,0:T(8,128)(2,1)S(1)} %copy-done.8, f32[1,4,128,1024]{3,2,1,0:T(8,128)S(1)} %bitcast.138, f32[4,1024]{1,0:T(4,128)S(1)} %get-tuple-element.24, f32[4,128]{1,0:T(4,128)S(1)} %multiply_bitcast_fusion, f32[4,1024]{1,0:T(4,128)S(1)} %fusion.71, f32[4,128]{1,0:T(4,128)S(1)} %copy-done.23, ...), kind=kLoop, calls=%fused_computation.17 | loop fusion | flops 6815744 | bytes 4237312 | tf_op jit(solution)/shard_map/convert_element_type | solution.py:228
  108.8 1.3 convolution_convert_fusion
  110.1 29.0 %shard_map.155 = (f32[32,1024]{1,0:T(8,128)S(1)}, bf16[512,1024]{1,0:T(8,128)(2,1)S(1)}, f32[4,1,128]{2,1,0:T(1,128)S(1)}) custom-call(bf16[4,4,2,32,1024]{4,3,2,1,0:T(8,128)(2,1)S(1)} %bitcast.136, bf16[16,1024]{1,0:T(8,128)(2,1)S(1)} %reshape.391.last_rows, f32[1,128]{1,0:T(1,128)S(1)} %broadcast_in_dim.45.loss_row), custom_call_target="tpu_custom_call" | custom-call | tf_op jit(solution)/shard_map/pallas_call | solution.py:569
  (118 shorter events, 16.5 us)
Async XLA Ops:
  0.6 7.8 %copy-start.7 = (bf16[1,4,128,1024]{3,2,1,0:T(8,128)(2,1)S(1)}, bf16[1,4,128,1024]{3,2,1,0:T(8,128)(2,1)}, u32[]{:S(2)}) copy-start(bf16[1,4,128,1024]{3,2,1,0:T(8,128)(2,1)} %param.10) | copy-start | bytes 3145732
  1.4 8.7 %copy-start.27 = (pred[4]{0:T(512)(128)(4,1)}, pred[4]{0:T(512)(128)(4,1)S(1)}, u32[]{:S(2)}) copy-start(pred[4]{0:T(512)(128)(4,1)S(1)} %compare_and_fusion) | copy-start | bytes 16
  4.9 3.6 %copy-start.20 = (f32[4,128]{1,0:T(4,128)}, f32[4,128]{1,0:T(4,128)S(1)}, u32[]{:S(2)}) copy-start(f32[4,128]{1,0:T(4,128)S(1)} %get-tuple-element.42) | copy-start | bytes 6148
  9.4 2.8 %copy-start.3 = (bf16[32,1024]{1,0:T(8,128)(2,1)S(1)}, bf16[32,1024]{1,0:T(8,128)(2,1)}, u32[]{:S(2)}) copy-start(bf16[32,1024]{1,0:T(8,128)(2,1)} %refs_0_.1) | copy-start | bytes 196612
  9.5 2.8 %copy-start.4 = (bf16[1024,32]{0,1:T(8,128)(2,1)S(1)}, bf16[1024,32]{0,1:T(8,128)(2,1)}, u32[]{:S(2)}) copy-start(bf16[1024,32]{0,1:T(8,128)(2,1)} %param.19) | copy-start | bytes 196612
  9.5 2.8 %copy-start.5 = (bf16[32,512]{1,0:T(8,128)(2,1)S(1)}, bf16[32,512]{1,0:T(8,128)(2,1)}, u32[]{:S(2)}) copy-start(bf16[32,512]{1,0:T(8,128)(2,1)} %refs_1_.1) | copy-start | bytes 98308
  9.5 2.7 %copy-start.6 = (bf16[32,512]{1,0:T(8,128)(2,1)S(1)}, bf16[32,512]{1,0:T(8,128)(2,1)}, u32[]{:S(2)}) copy-start(bf16[32,512]{1,0:T(8,128)(2,1)} %refs_2_.1) | copy-start | bytes 98308
  10.8 44.5 %copy-start.16 = (f32[1024]{0:T(1024)S(1)}, f32[1024]{0:T(1024)}, u32[]{:S(2)}) copy-start(f32[1024]{0:T(1024)} %param.13) | copy-start | bytes 12292
  51.7 1.3 copy-start
  53.0 1.0 copy-start.1
  55.3 5.4 %copy-start.21 = (f32[4,128]{1,0:T(4,128)S(1)}, f32[4,128]{1,0:T(4,128)}, u32[]{:S(2)}) copy-start(f32[4,128]{1,0:T(4,128)} %copy-done.20) | copy-start | bytes 6148
  63.0 1.0 copy-start.9
  63.1 0.9 copy-start.14
  65.0 2.6 %copy-start.28 = (pred[4]{0:T(512)(128)(4,1)S(1)}, pred[4]{0:T(512)(128)(4,1)}, u32[]{:S(2)}) copy-start(pred[4]{0:T(512)(128)(4,1)} %copy-done.27) | copy-start | bytes 16
  67.6 2.6 %copy-start.25 = (f32[4,128]{1,0:T(4,128)S(1)}, f32[4,128]{1,0:T(4,128)}, u32[]{:S(2)}) copy-start(f32[4,128]{1,0:T(4,128)} %fusion.49) | copy-start | bytes 6148
  67.6 2.6 %copy-start.26 = (f32[4,128]{1,0:T(4,128)S(1)}, f32[4,128]{1,0:T(4,128)}, u32[]{:S(2)}) copy-start(f32[4,128]{1,0:T(4,128)} %fusion.48) | copy-start | bytes 6148
  67.6 2.7 %copy-start.13 = (bf16[4,128,4,128]{1,3,2,0:T(8,128)(2,1)S(1)}, bf16[4,128,4,128]{1,3,2,0:T(8,128)(2,1)}, u32[]{:S(2)}) copy-start(bf16[4,128,4,128]{1,3,2,0:T(8,128)(2,1)} %fusion.19) | copy-start | bytes 1572868
  67.6 2.7 %copy-start.29 = (pred[4,128]{1,0:T(4,128)(4,1)S(1)}, pred[4,128]{1,0:T(4,128)(4,1)}, u32[]{:S(2)}) copy-start(pred[4,128]{1,0:T(4,128)(4,1)} %get-tuple-element.45) | copy-start | bytes 1540
  67.6 4.3 %copy-start.15 = (f32[4,1024]{1,0:T(4,128)S(1)}, f32[4,1024]{1,0:T(4,128)}, u32[]{:S(2)}) copy-start(f32[4,1024]{1,0:T(4,128)} %gather_fusion) | copy-start | bytes 49156
  70.0 4.3 %copy-start.17 = (f32[1024]{0:T(1024)S(1)}, f32[1024]{0:T(1024)}, u32[]{:S(2)}) copy-start(f32[1024]{0:T(1024)} %param.15) | copy-start | bytes 12292
  70.0 4.4 %copy-start.18 = (f32[1024]{0:T(1024)S(1)}, f32[1024]{0:T(1024)}, u32[]{:S(2)}) copy-start(f32[1024]{0:T(1024)} %param.14) | copy-start | bytes 12292
  70.1 4.5 %copy-start.31 = (f32[1,4]{1,0:T(1,128)S(1)}, f32[1,4]{1,0:T(1,128)}, u32[]{:S(2)}) copy-start(f32[1,4]{1,0:T(1,128)} %param.12) | copy-start | bytes 52
  74.6 22.0 %copy-start.30 = (f32[4]{0:T(128)}, f32[4]{0:T(128)S(1)}, u32[]{:S(2)}) copy-start(f32[4]{0:T(128)S(1)} %multiply_reduce_fusion.6) | copy-start | bytes 52
  92.3 4.2 %copy-start.19 = (bf16[4,1024]{1,0:T(4,128)(2,1)S(1)}, bf16[4,1024]{1,0:T(4,128)(2,1)}, u32[]{:S(2)}) copy-start(bf16[4,1024]{1,0:T(4,128)(2,1)} %broadcast_select_fusion) | copy-start | bytes 24580
  98.2 1.2 copy-start.10
  99.7 3.3 %copy-start.2 = (bf16[1024,512]{1,0:T(8,128)(2,1)S(1)}, bf16[1024,512]{1,0:T(8,128)(2,1)}, u32[]{:S(2)}) copy-start(bf16[1024,512]{1,0:T(8,128)(2,1)} %copy-done.1) | copy-start | bytes 3145732
  103.0 1.9 %copy-start.8 = (bf16[1,4,128,1024]{3,2,1,0:T(8,128)(2,1)S(1)}, bf16[1,4,128,1024]{3,2,1,0:T(8,128)(2,1)}, u32[]{:S(2)}) copy-start(bf16[1,4,128,1024]{3,2,1,0:T(8,128)(2,1)} %param.10) | copy-start | bytes 3145732
  103.0 1.9 %copy-start.11 = (bf16[4,128,4,128]{3,2,1,0:T(4,128)(2,1)S(1)}, bf16[4,128,4,128]{3,2,1,0:T(4,128)(2,1)}, u32[]{:S(2)}) copy-start(bf16[4,128,4,128]{3,2,1,0:T(4,128)(2,1)} %copy.32) | copy-start | bytes 1572868
  103.0 1.9 %copy-start.22 = (f32[512]{0:T(512)S(1)}, f32[512]{0:T(512)}, u32[]{:S(2)}) copy-start(f32[512]{0:T(512)} %get-tuple-element.41) | copy-start | bytes 6148
  103.0 2.0 %copy-start.24 = (f32[512]{0:T(512)S(1)}, f32[512]{0:T(512)}, u32[]{:S(2)}) copy-start(f32[512]{0:T(512)} %get-tuple-element.44) | copy-start | bytes 6148
  104.9 1.2 copy-start.23
  106.2 2.5 %copy-start.12 = (bf16[4,128,4,128]{3,2,1,0:T(4,128)(2,1)S(1)}, bf16[4,128,4,128]{3,2,1,0:T(4,128)(2,1)}, u32[]{:S(2)}) copy-start(bf16[4,128,4,128]{3,2,1,0:T(4,128)(2,1)} %copy.31) | copy-start | bytes 1572868
